TPU v7x, 256 devices: a 8x8x2 block of a 8x8x16 slice. The times are simulated.
256 devices in a mesh: slab: 2 (over z), wide: 128 (over x, y, core).
Axes of the slice: x: 8, y: 8, z: 2, core: 2. Of those that a mesh axis runs over, the one named last changes fastest.
The devices are a block of a 8x8x16 slice.
Arguments:
- slc: bfloat16 [128, 4096, 2, 512], P('wide', 'slab'), parts along dimension 1, may hold values from -10 to 10
- offsets: bfloat16 [128, 4096], P('wide', 'slab'), parts along dimension 1, may hold values from -0.5 to 0.5
- row_start: int32 [128], replicated, may hold values from 0 to 127
- row_stop: int32 [128], replicated, may hold values from 385 to 512
- pairs: int32 [512, 2], replicated, may hold values from 0 to 127, as said below
Outputs:
- coherence: bfloat16 [8192, 2, 128, 128], P(('slab', 'wide')), parts along dimension 0
- flattened: float32 [8192, 2, 512], P(('slab', 'wide')), parts along dimension 0
- ramps: float32 [1024, 2, 3], P(('slab', 'wide')), parts along dimension 0
There are 2 independent parts, one for each index of `slab`. A program takes and returns all parts, laid end to end along the dimension named above; an argument that names none is the same for every part. Nothing has to cross between parts.
Inputs may be any that keep to these rules, and one draw needn't show every extreme that they name: `pairs`: each row names two different dates.
All inputs are finite; a program needn't handle non-finite values.
Results may differ from a plain program's by a relative error of at most 0.0098.
Values may be sent and summed in bfloat16 or wider, within the bound.
No kernel may reach another device: no remote copies, remote signals or barrier semaphores. Data moves between devices by JAX's collectives and lax.ppermute only.
A program may use at most 128 MiB of HBM per device.

v0:
```python
import math

import jax
import jax.numpy as jnp
from jax import lax
from jax.experimental import pallas as pl
from jax.experimental.pallas import tpu as pltpu
from jax.sharding import Mesh
from jax.sharding import PartitionSpec as P

AZ = 512
LOOK_AZ = 16
LOOK_RG = 16
LINE_CELLS = AZ // LOOK_AZ
WIDE = ("wide_0", "wide_1", "wide_2")
SLAB_WIDE = ("slab", "wide_0", "wide_1", "wide_2")
DAMPING = 1.0
COLS_STEP = 4
CELLS_STEP = 4
ROT_ROWS = 16


def spectral_table():
    ordinal = jnp.arange(AZ, dtype=jnp.int32)
    product = ordinal[:, None] * ordinal[None, :] % AZ
    angles = product.astype(jnp.float32) * (2.0 * math.pi / AZ)
    cosine = jnp.cos(angles).astype(jnp.bfloat16)
    sine = jnp.sin(angles).astype(jnp.bfloat16)
    return jnp.concatenate(
        [jnp.concatenate([cosine, -sine], 1), jnp.concatenate([sine, cosine], 1)], 0
    )


def exchange_small(rows):
    count = rows.shape[0]
    index = jnp.arange(count, dtype=jnp.int32)[:, None]
    stride = 1
    for axis in reversed(WIDE):
        size = lax.axis_size(axis)
        own = lax.axis_index(axis)
        step = 1
        while step < size:
            bit = (own // step) % 2
            got = lax.ppermute(rows, axis, [(i, i ^ step) for i in range(size)])
            got = jnp.where(bit == 0, jnp.roll(got, stride, 0), jnp.roll(got, -stride, 0))
            rows = jnp.where((index // stride) % 2 == bit, rows, got)
            stride *= 2
            step *= 2
    return rows


def rotated(spectrum, shift, frequency):
    z = frequency * shift
    zz = z * z
    sin_rot = z * (
        1.0
        + zz
        * (
            -1.0 / 6
            + zz * (1.0 / 120 + zz * (-1.0 / 5040 + zz * (1.0 / 362880 + zz * (-1.0 / 39916800))))
        )
    )
    cos_rot = 1.0 + zz * (
        -0.5
        + zz
        * (
            1.0 / 24
            + zz
            * (
                -1.0 / 720
                + zz * (1.0 / 40320 + zz * (-1.0 / 3628800 + zz * (1.0 / 479001600)))
            )
        )
    )
    real, imag = spectrum[:, :AZ], spectrum[:, AZ:]
    return jnp.concatenate(
        [real * cos_rot - imag * sin_rot, real * sin_rot + imag * cos_rot], 1
    )


def cells_kernel(
    x_ref, valid_ref, shift_ref, table_ref, second_ref, first_ref, coh_ref, ifg_ref, sums_ref,
    spec_ref, turned_ref, pix_ref, int_ref,
):
    step = pl.program_id(0)
    dates = valid_ref.shape[0]
    range_steps = LOOK_RG // COLS_STEP

    @pl.when(step < range_steps)
    def _resample():
        valid = valid_ref[...]
        parts = []
        for part in range(2):
            parts.append(
                jnp.concatenate([x_ref[c, part] * valid for c in range(COLS_STEP)], 0)
            )
        stacked = jnp.concatenate(parts, 1)
        spec_ref[...] = jnp.dot(
            stacked, table_ref[...], preferred_element_type=jnp.float32
        ).astype(jnp.bfloat16)
        bins = lax.broadcasted_iota(jnp.int32, (1, AZ), 1)
        frequency = jnp.where(bins < AZ // 2, bins, bins - AZ).astype(jnp.float32)
        frequency = frequency * (-2.0 * math.pi / AZ)

        def turn(i, _):
            rows = pl.ds(pl.multiple_of(i * ROT_ROWS, ROT_ROWS), ROT_ROWS)
            turned_ref[rows, :] = rotated(
                spec_ref[rows, :].astype(jnp.float32), shift_ref[rows, :], frequency
            ).astype(jnp.bfloat16)
            return _

        lax.fori_loop(0, COLS_STEP * dates // ROT_ROWS, turn, None)
        restored = lax.dot_general(
            table_ref[...], turned_ref[...], (((1,), (1,)), ((), ())),
            preferred_element_type=jnp.float32,
        )
        restored = (restored * (1.0 / AZ)).astype(jnp.bfloat16)
        for c in range(COLS_STEP):
            pix_ref[:, :, step * COLS_STEP + c] = restored[
                :, c * dates : (c + 1) * dates
            ].reshape(2, LINE_CELLS, LOOK_AZ, dates)

    @pl.when(step >= range_steps)
    def _covariance():
        diagonal = lax.broadcasted_iota(jnp.int32, (dates, dates), 0) == lax.broadcasted_iota(
            jnp.int32, (dates, dates), 1
        )
        base = (step - range_steps) * CELLS_STEP

        def cell_of(k, _):
            cell = base + k
            real = pix_ref[0, cell].reshape(LOOK_RG * LOOK_AZ, dates)
            imag = pix_ref[1, cell].reshape(LOOK_RG * LOOK_AZ, dates)
            pixels = jnp.concatenate([real, imag], 0)
            partner = jnp.concatenate([pixels, jnp.concatenate([-imag, real], 0)], 1)
            cov = lax.dot_general(
                pixels, partner, (((0,), (0,)), ((), ())), preferred_element_type=jnp.float32
            )
            on_diagonal = jnp.where(diagonal, cov[:, :dates], 0.0)
            scale_rows = lax.rsqrt(jnp.sum(on_diagonal, 1, keepdims=True) + DAMPING)
            scale_cols = lax.rsqrt(jnp.sum(on_diagonal, 0, keepdims=True) + DAMPING)
            scale = scale_rows * scale_cols
            gamma = jnp.concatenate([cov[:, :dates] * scale, cov[:, dates:] * scale], 0)
            high = gamma.astype(jnp.bfloat16)
            coh_ref[k] = high.reshape(2, dates, dates)
            low = (gamma - high.astype(jnp.float32)).astype(jnp.bfloat16)
            picked = jnp.dot(
                jnp.concatenate([high, low], 1), second_ref[...], preferred_element_type=jnp.float32
            )
            first = first_ref[...]
            int_ref[cell, 0:1, :] = jnp.sum(picked[:dates] * first, 0, keepdims=True)
            int_ref[cell, 1:2, :] = jnp.sum(picked[dates:] * first, 0, keepdims=True)
            return _

        lax.fori_loop(0, CELLS_STEP, cell_of, None)

    @pl.when(step == pl.num_programs(0) - 1)
    def _sums():
        ifg = int_ref[...]
        ifg_ref[...] = ifg
        real, imag = ifg[:, 0, :], ifg[:, 1, :]
        weight = 0.1 + real * real + imag * imag
        across = (lax.broadcasted_iota(jnp.int32, (LINE_CELLS, 1), 0).astype(jnp.float32) + 0.5) / LINE_CELLS - 0.5
        tilted = weight * across
        terms = (weight, tilted, tilted * across, weight * real, tilted * real, weight * imag, tilted * imag)
        for k, term in enumerate(terms):
            sums_ref[k : k + 1, :] = jnp.sum(term, 0, keepdims=True)
        sums_ref[len(terms) :, :] = jnp.zeros_like(sums_ref[len(terms) :, :])


def cells_call(x, valid, shifts, table, second, first):
    dates = valid.shape[0]
    pairs = first.shape[1]
    range_steps = LOOK_RG // COLS_STEP
    steps = range_steps + LINE_CELLS // CELLS_STEP
    last = range_steps - 1
    whole = lambda *shape: pl.BlockSpec(shape, lambda s: (0,) * len(shape))
    rows = COLS_STEP * dates
    return pl.pallas_call(
        cells_kernel,
        grid=(steps,),
        in_specs=[
            pl.BlockSpec((COLS_STEP, 2, dates, AZ), lambda s: (jnp.minimum(s, last), 0, 0, 0)),
            whole(dates, AZ),
            pl.BlockSpec((rows, 1), lambda s: (jnp.minimum(s, last), 0)),
            whole(2 * AZ, 2 * AZ),
            whole(2 * dates, pairs),
            whole(dates, pairs),
        ],
        out_specs=[
            pl.BlockSpec(
                (CELLS_STEP, 2, dates, dates), lambda s: (jnp.maximum(s - range_steps, 0), 0, 0, 0)
            ),
            whole(LINE_CELLS, 2, pairs),
            whole(8, pairs),
        ],
        out_shape=[
            jax.ShapeDtypeStruct((LINE_CELLS, 2, dates, dates), jnp.bfloat16),
            jax.ShapeDtypeStruct((LINE_CELLS, 2, pairs), jnp.float32),
            jax.ShapeDtypeStruct((8, pairs), jnp.float32),
        ],
        scratch_shapes=[
            pltpu.VMEM((rows, 2 * AZ), jnp.bfloat16),
            pltpu.VMEM((rows, 2 * AZ), jnp.bfloat16),
            pltpu.VMEM((2, LINE_CELLS, LOOK_RG, LOOK_AZ, dates), jnp.bfloat16),
            pltpu.VMEM((LINE_CELLS, 2, pairs), jnp.float32),
        ],
        compiler_params=pltpu.CompilerParams(dimension_semantics=("arbitrary",)),
        name="cells",
    )(x, valid, shifts, table, second, first)


def plane_sums(gathered, first_range, range_cells):
    along = (first_range + jnp.arange(gathered.shape[0], dtype=jnp.int32)).astype(jnp.float32)
    along = ((along + 0.5) / range_cells - 0.5)[:, None]
    w0, w1, w2, r0, r1, i0, i1 = (gathered[:, k] for k in range(7))
    terms = (w0, w1, w0 * along, w2, w1 * along, w0 * along * along, r0, r1, r0 * along, i0, i1, i0 * along)
    return jnp.stack([jnp.sum(t, 0) for t in terms], 0)


def solve_three(n):
    adjugate_00 = n[3] * n[5] - n[4] * n[4]
    adjugate_01 = n[2] * n[4] - n[1] * n[5]
    adjugate_02 = n[1] * n[4] - n[2] * n[3]
    adjugate_11 = n[0] * n[5] - n[2] * n[2]
    adjugate_12 = n[1] * n[2] - n[0] * n[4]
    adjugate_22 = n[0] * n[3] - n[1] * n[1]
    determinant = n[0] * adjugate_00 + n[1] * adjugate_01 + n[2] * adjugate_02
    parts = []
    for t in (n[6:9], n[9:12]):
        parts.append(
            jnp.stack(
                [
                    adjugate_00 * t[0] + adjugate_01 * t[1] + adjugate_02 * t[2],
                    adjugate_01 * t[0] + adjugate_11 * t[1] + adjugate_12 * t[2],
                    adjugate_02 * t[0] + adjugate_12 * t[1] + adjugate_22 * t[2],
                ],
                0,
            )
            / determinant
        )
    return jnp.stack(parts, 0)


def shared_by_all(array, axes):
    size = 1
    for a in (axes if isinstance(axes, tuple) else (axes,)):
        size *= lax.axis_size(a)
    copies = jnp.broadcast_to(array[None], (size, *array.shape))
    return lax.all_to_all(copies, axes, 0, 0, tiled=True)


def local(slc, offsets, row_start, row_stop, pairs):
    devices = lax.axis_size(WIDE)
    position = lax.axis_index(WIDE)
    columns = slc.shape[1]
    dates = devices * slc.shape[0]
    received = lax.all_to_all(
        slc.reshape(devices, columns // devices, 2, AZ), WIDE, 0, 0, tiled=True
    )
    x = received.transpose(1, 2, 0, 3)
    shifts = exchange_small(offsets.reshape(devices, columns // devices))
    shifts = shifts.astype(jnp.float32).T.reshape(-1, 1)
    lines = jnp.arange(AZ, dtype=jnp.int32)[None, :]
    valid = ((lines >= row_start[:, None]) & (lines < row_stop[:, None])).astype(jnp.bfloat16)
    date = jnp.arange(dates, dtype=jnp.int32)[:, None]
    first = (date == pairs[:, 0][None, :]).astype(jnp.float32)
    second = (date == pairs[:, 1][None, :]).astype(jnp.bfloat16)
    second = jnp.concatenate([second, second], 0)
    coherence, ifg, sums = cells_call(x, valid, shifts, spectral_table(), second, first)

    range_cells = columns // LOOK_RG
    near = lax.axis_size(("wide_1", "wide_2"))
    gathered = shared_by_all(sums, ("wide_1", "wide_2"))
    partial = plane_sums(gathered, lax.axis_index("wide_0") * near, range_cells)
    total = jnp.sum(shared_by_all(partial, "wide_0"), 0)
    ramps = solve_three(total)
    share = pairs.shape[0] // devices
    own = lax.dynamic_slice_in_dim(ramps, position * share, share, 2).transpose(2, 0, 1)
    across = (jnp.arange(LINE_CELLS, dtype=jnp.int32).astype(jnp.float32) + 0.5) / LINE_CELLS - 0.5
    along = (position.astype(jnp.float32) + 0.5) / range_cells - 0.5
    plane = ramps[:, 0] + across[:, None, None] * ramps[:, 1] + along * ramps[:, 2]
    return coherence, ifg - plane, own


def solution(mesh):
    torus = Mesh(
        mesh.devices.reshape(mesh.shape["slab"], 8, 8, 2), ("slab", "wide_0", "wide_1", "wide_2")
    )
    in_specs = (P(WIDE, "slab", None, None), P(WIDE, "slab"), P(), P(), P())
    out_specs = (P(SLAB_WIDE, None, None, None), P(SLAB_WIDE, None, None), P(SLAB_WIDE, None, None))
    return jax.shard_map(local, mesh=torus, in_specs=in_specs, out_specs=out_specs, check_vma=False)
```

profile of v0, /device:TPU:513, one launch (start us, length us, event | category | flops | bytes accessed | tf_op | source)
XLA Modules:
  0.0 250.7 jit_solution(6522771041306525066)
XLA Ops:
  0.6 0.0 copy-start
  0.6 0.0 copy-start.1
  0.7 28.6 %all-to-all-start = ((bf16[128,16,2,512]{3,2,1,0:T(2,128)(2,1)}), bf16[128,16,2,512]{3,2,1,0:T(2,128)(2,1)}, u32[]{:S(2)}, u32[]{:S(2)}) async-start(bf16[128,16,2,512]{3,2,1,0:T(2,128)(2,1)} %bitcast.67), calls=%async_computation | async-start | bytes 8388608 | tf_op jit(solution)/shard_map/all_to_all | solution.py:258
  29.3 0.0 copy-start.2
  29.3 0.0 copy-start.3
  29.3 0.1 reshape.523
  29.4 3.1 %collective-permute-start = (bf16[128,16]{1,0:T(8,128)(2,1)S(1)}, bf16[128,16]{1,0:T(8,128)(2,1)S(1)}, u32[]{:S(2)}, u32[]{:S(2)}) collective-permute-start(bf16[128,16]{1,0:T(8,128)(2,1)S(1)} %reshape.523), channel_id=1, source_target_pairs={{0,1},{1,0},{2,3},{3,2},{4,5},{5,4},{6,7},{7,6},{8,9},{9,8},{10,11... | collective-permute-start | bytes 12296 | tf_op jit(solution)/shard_map/ppermute | solution.py:44
  32.6 0.7 add_convert_fusion.second_ref
  33.3 4.0 %fusion.9 = bf16[512,512]{1,0:T(8,128)(2,1)S(1)} fusion(), kind=kLoop, calls=%fused_computation.21 | loop fusion | flops 4718592 | bytes 524288 | tf_op jit(solution)/shard_map/neg | solution.py:30
  37.3 4.3 %sine_convert_fusion = (bf16[512,512]{1,0:T(8,128)(2,1)S(1)}, bf16[512,512]{1,0:T(8,128)(2,1)S(1)}) fusion(), kind=kLoop, calls=%fused_computation.8 | loop fusion | flops 4194304 | bytes 1048576 | tf_op jit(solution)/shard_map/convert_element_type | solution.py:28
  41.6 1.7 maximum_maximum_fusion.table_ref
  43.3 0.8 fusion.7
  44.1 0.0 collective-permute-done
  44.1 0.1 fusion.10
  44.2 0.1 collective-permute-start.1
  44.4 35.7 %collective-permute-done.1 = bf16[128,16]{1,0:T(8,128)(2,1)S(1)} collective-permute-done((bf16[128,16]{1,0:T(8,128)(2,1)S(1)}, bf16[128,16]{1,0:T(8,128)(2,1)S(1)}, u32[]{:S(2)}, u32[]{:S(2)}) %collective-permute-start.1) | collective-permute-done | bytes 4128 | tf_op jit(solution)/shard_map/ppermute | solution.py:44
  80.1 0.1 fusion.11
  80.2 0.3 collective-permute-start.2
  80.5 37.5 %collective-permute-done.2 = bf16[128,16]{1,0:T(8,128)(2,1)S(1)} collective-permute-done((bf16[128,16]{1,0:T(8,128)(2,1)S(1)}, bf16[128,16]{1,0:T(8,128)(2,1)S(1)}, u32[]{:S(2)}, u32[]{:S(2)}) %collective-permute-start.2) | collective-permute-done | bytes 4128 | tf_op jit(solution)/shard_map/ppermute | solution.py:44
  118.0 0.1 fusion.12
  118.1 11.5 %collective-permute-start.3 = (bf16[128,16]{1,0:T(8,128)(2,1)S(1)}, bf16[128,16]{1,0:T(8,128)(2,1)S(1)}, u32[]{:S(2)}, u32[]{:S(2)}) collective-permute-start(bf16[128,16]{1,0:T(8,128)(2,1)S(1)} %fusion.12), channel_id=1, source_target_pairs={{0,8},{2,10},{4,12},{6,14},{8,0},{10,2},{12,4},{14,6},{1,9},{3,11}... | collective-permute-start | bytes 12296 | tf_op jit(solution)/shard_map/ppermute | solution.py:44
  129.6 1.4 collective-permute-done.3
  131.0 0.1 fusion.13
  131.1 2.4 collective-permute-start.4
  133.5 1.3 collective-permute-done.4
  134.8 0.1 fusion.14
  134.9 6.5 %collective-permute-start.5 = (bf16[128,16]{1,0:T(8,128)(2,1)S(1)}, bf16[128,16]{1,0:T(8,128)(2,1)S(1)}, u32[]{:S(2)}, u32[]{:S(2)}) collective-permute-start(bf16[128,16]{1,0:T(8,128)(2,1)S(1)} %fusion.14), channel_id=1, source_target_pairs={{0,32},{16,48},{32,0},{48,16},{64,96},{80,112},{96,64},{112,80},{1... | collective-permute-start | bytes 12296 | tf_op jit(solution)/shard_map/ppermute | solution.py:44
  141.4 1.3 collective-permute-done.5
  142.7 0.1 fusion.15
  142.8 4.8 %collective-permute-start.6 = (bf16[128,16]{1,0:T(8,128)(2,1)S(1)}, bf16[128,16]{1,0:T(8,128)(2,1)S(1)}, u32[]{:S(2)}, u32[]{:S(2)}) collective-permute-start(bf16[128,16]{1,0:T(8,128)(2,1)S(1)} %fusion.15), channel_id=1, source_target_pairs={{0,64},{16,80},{32,96},{48,112},{64,0},{80,16},{96,32},{112,48},{1... | collective-permute-start | bytes 12296 | tf_op jit(solution)/shard_map/ppermute | solution.py:44
  147.7 2.1 collective-permute-done.6
  149.8 0.1 convert_bitcast_fusion
  149.9 0.1 copy.75
  150.0 1.4 copy.76.shift_ref
  151.3 0.0 all-to-all-done
  151.3 6.5 %copy.129 = bf16[128,16,2,512]{3,0,2,1:T(8,128)(2,1)} copy(bf16[128,16,2,512]{3,2,1,0:T(2,128)(2,1)} %all-to-all-done) | data formatting | bytes 8388608 | tf_op jit(solution)/shard_map/all_to_all | solution.py:258
  157.8 43.4 %cells.1 = (bf16[32,2,128,128]{3,2,1,0:T(8,128)(2,1)}, f32[32,2,512]{2,1,0:T(2,128)}, f32[8,512]{1,0:T(8,128)}) custom-call(bf16[16,2,128,512]{3,2,1,0:T(8,128)(2,1)} %bitcast.66, bf16[128,512]{1,0:T(8,128)(2,1)} %get-tuple-element.81.valid_ref, f32[2048,1]{1,0:T(8,128)} %copy.76.shift_ref, bf16[1024,1024]{1,0:T(8,128)(2,1)} %maximum_maximum_fusion.table_ref, ...), custom_call_target="tpu_custom_call" | custom-call | tf_op jit(solution)/shard_map/cells/pallas_call | solution.py:179
  201.2 1.4 broadcast_in_dim.69
  202.6 13.4 %all-to-all-start.1 = ((f32[16,8,512]{2,1,0:T(8,128)}), f32[16,8,512]{2,1,0:T(8,128)S(1)}, u32[]{:S(2)}, u32[]{:S(2)}) async-start(f32[16,8,512]{2,1,0:T(8,128)} %broadcast_in_dim.69), calls=%async_computation.1 | async-start | bytes 524288 | tf_op jit(solution)/shard_map/all_to_all | solution.py:250
  216.1 11.6 %all-to-all-done.1 = f32[16,8,512]{2,1,0:T(8,128)S(1)} async-done(((f32[16,8,512]{2,1,0:T(8,128)}), f32[16,8,512]{2,1,0:T(8,128)S(1)}, u32[]{:S(2)}, u32[]{:S(2)}) %all-to-all-start.1) | async-done | bytes 262176 | tf_op jit(solution)/shard_map/all_to_all | solution.py:250
  227.6 0.3 fusion.44
  227.9 0.1 fusion.21
  228.0 0.1 stack.80
  228.1 0.7 broadcast_in_dim.70
  228.8 6.9 %all-to-all-start.2 = ((f32[8,12,512]{2,1,0:T(8,128)}), f32[8,12,512]{2,1,0:T(8,128)S(1)}, u32[]{:S(2)}, u32[]{:S(2)}) async-start(f32[8,12,512]{2,1,0:T(8,128)} %broadcast_in_dim.70), calls=%async_computation.2 | async-start | bytes 524288 | tf_op jit(solution)/shard_map/all_to_all | solution.py:250
  235.7 12.4 %all-to-all-done.2 = f32[8,12,512]{2,1,0:T(8,128)S(1)} async-done(((f32[8,12,512]{2,1,0:T(8,128)}), f32[8,12,512]{2,1,0:T(8,128)S(1)}, u32[]{:S(2)}, u32[]{:S(2)}) %all-to-all-start.2) | async-done | bytes 196640 | tf_op jit(solution)/shard_map/all_to_all | solution.py:250
  248.3 0.7 fusion.29
  249.0 1.7 add_subtract_fusion
  (36 shorter events, 0.4 us)
Async XLA Ops:
  0.6 28.6 %copy-start = (bf16[1,2048]{1,0:T(2,128)(2,1)S(1)}, bf16[1,2048]{1,0:T(2,128)(2,1)}, u32[]{:S(2)}) copy-start(bf16[1,2048]{1,0:T(2,128)(2,1)} %param.6) | copy-start | bytes 12292
  0.6 31.9 %copy-start.1 = (s32[512,2]{0,1:T(2,128)S(1)}, s32[512,2]{0,1:T(2,128)}, u32[]{:S(2)}) copy-start(s32[512,2]{0,1:T(2,128)} %param.9) | copy-start | bytes 12292
  0.7 150.7 %all-to-all-start = ((bf16[128,16,2,512]{3,2,1,0:T(2,128)(2,1)}), bf16[128,16,2,512]{3,2,1,0:T(2,128)(2,1)}, u32[]{:S(2)}, u32[]{:S(2)}) async-start(bf16[128,16,2,512]{3,2,1,0:T(2,128)(2,1)} %bitcast.67), calls=%async_computation | async-start | bytes 8388608 | tf_op jit(solution)/shard_map/all_to_all | solution.py:258
  29.3 14.0 %copy-start.2 = (s32[128]{0:T(128)S(1)}, s32[128]{0:T(128)}, u32[]{:S(2)}) copy-start(s32[128]{0:T(128)} %param.8) | copy-start | bytes 1540
  29.3 14.0 %copy-start.3 = (s32[128]{0:T(128)S(1)}, s32[128]{0:T(128)}, u32[]{:S(2)}) copy-start(s32[128]{0:T(128)} %param.7) | copy-start | bytes 1540
  29.4 14.7 %collective-permute-start = (bf16[128,16]{1,0:T(8,128)(2,1)S(1)}, bf16[128,16]{1,0:T(8,128)(2,1)S(1)}, u32[]{:S(2)}, u32[]{:S(2)}) collective-permute-start(bf16[128,16]{1,0:T(8,128)(2,1)S(1)} %reshape.523), channel_id=1, source_target_pairs={{0,1},{1,0},{2,3},{3,2},{4,5},{5,4},{6,7},{7,6},{8,9},{9,8},{10,11... | collective-permute-start | bytes 12296 | tf_op jit(solution)/shard_map/ppermute | solution.py:44
  44.2 35.9 %collective-permute-start.1 = (bf16[128,16]{1,0:T(8,128)(2,1)S(1)}, bf16[128,16]{1,0:T(8,128)(2,1)S(1)}, u32[]{:S(2)}, u32[]{:S(2)}) collective-permute-start(bf16[128,16]{1,0:T(8,128)(2,1)S(1)} %fusion.10), channel_id=1, source_target_pairs={{0,2},{2,0},{4,6},{6,4},{8,10},{10,8},{12,14},{14,12},{1,3},{3,1},... | collective-permute-start | bytes 12296 | tf_op jit(solution)/shard_map/ppermute | solution.py:44
  80.2 37.8 %collective-permute-start.2 = (bf16[128,16]{1,0:T(8,128)(2,1)S(1)}, bf16[128,16]{1,0:T(8,128)(2,1)S(1)}, u32[]{:S(2)}, u32[]{:S(2)}) collective-permute-start(bf16[128,16]{1,0:T(8,128)(2,1)S(1)} %fusion.11), channel_id=1, source_target_pairs={{0,4},{2,6},{4,0},{6,2},{8,12},{10,14},{12,8},{14,10},{1,5},{3,7},... | collective-permute-start | bytes 12296 | tf_op jit(solution)/shard_map/ppermute | solution.py:44
  118.1 12.9 %collective-permute-start.3 = (bf16[128,16]{1,0:T(8,128)(2,1)S(1)}, bf16[128,16]{1,0:T(8,128)(2,1)S(1)}, u32[]{:S(2)}, u32[]{:S(2)}) collective-permute-start(bf16[128,16]{1,0:T(8,128)(2,1)S(1)} %fusion.12), channel_id=1, source_target_pairs={{0,8},{2,10},{4,12},{6,14},{8,0},{10,2},{12,4},{14,6},{1,9},{3,11}... | collective-permute-start | bytes 12296 | tf_op jit(solution)/shard_map/ppermute | solution.py:44
  131.1 3.7 %collective-permute-start.4 = (bf16[128,16]{1,0:T(8,128)(2,1)S(1)}, bf16[128,16]{1,0:T(8,128)(2,1)S(1)}, u32[]{:S(2)}, u32[]{:S(2)}) collective-permute-start(bf16[128,16]{1,0:T(8,128)(2,1)S(1)} %fusion.13), channel_id=1, source_target_pairs={{0,16},{16,0},{32,48},{48,32},{64,80},{80,64},{96,112},{112,96},{1... | collective-permute-start | bytes 12296 | tf_op jit(solution)/shard_map/ppermute | solution.py:44
  134.9 7.8 %collective-permute-start.5 = (bf16[128,16]{1,0:T(8,128)(2,1)S(1)}, bf16[128,16]{1,0:T(8,128)(2,1)S(1)}, u32[]{:S(2)}, u32[]{:S(2)}) collective-permute-start(bf16[128,16]{1,0:T(8,128)(2,1)S(1)} %fusion.14), channel_id=1, source_target_pairs={{0,32},{16,48},{32,0},{48,16},{64,96},{80,112},{96,64},{112,80},{1... | collective-permute-start | bytes 12296 | tf_op jit(solution)/shard_map/ppermute | solution.py:44
  142.8 7.0 %collective-permute-start.6 = (bf16[128,16]{1,0:T(8,128)(2,1)S(1)}, bf16[128,16]{1,0:T(8,128)(2,1)S(1)}, u32[]{:S(2)}, u32[]{:S(2)}) collective-permute-start(bf16[128,16]{1,0:T(8,128)(2,1)S(1)} %fusion.15), channel_id=1, source_target_pairs={{0,64},{16,80},{32,96},{48,112},{64,0},{80,16},{96,32},{112,48},{1... | collective-permute-start | bytes 12296 | tf_op jit(solution)/shard_map/ppermute | solution.py:44
  202.6 25.0 %all-to-all-start.1 = ((f32[16,8,512]{2,1,0:T(8,128)}), f32[16,8,512]{2,1,0:T(8,128)S(1)}, u32[]{:S(2)}, u32[]{:S(2)}) async-start(f32[16,8,512]{2,1,0:T(8,128)} %broadcast_in_dim.69), calls=%async_computation.1 | async-start | bytes 524288 | tf_op jit(solution)/shard_map/all_to_all | solution.py:250
  228.8 19.3 %all-to-all-start.2 = ((f32[8,12,512]{2,1,0:T(8,128)}), f32[8,12,512]{2,1,0:T(8,128)S(1)}, u32[]{:S(2)}, u32[]{:S(2)}) async-start(f32[8,12,512]{2,1,0:T(8,128)} %broadcast_in_dim.70), calls=%async_computation.2 | async-start | bytes 524288 | tf_op jit(solution)/shard_map/all_to_all | solution.py:250
where the time goes:
time: 251 us
  waiting for transfers between devices  103 us (41%)
  starting transfers between devices  77.7 us (31%)
  Pallas kernels  43.4 us (17%)
  other arithmetic  15.2 us (6%)
  local copies, waits for them, and re-layouts  10.3 us (4%)
    ppermute x7, waiting for transfers between devices, exchange_small(): got = lax.ppermute(rows, axis, [(i, i ^ step) for i in range(size)])  79.3 us
    pallas_call x1, Pallas kernels, cells_call(): pl.pallas_call(cells_kernel, grid=(steps,), in_specs=[pl.BlockSpec((COLS_...  43.4 us
    ppermute x7, starting transfers between devices, exchange_small(): got = lax.ppermute(rows, axis, [(i, i ^ step) for i in range(size)])  28.7 us
    all_to_all x1, starting transfers between devices, local(): lax.all_to_all(slc.reshape(devices, columns // devices, 2, AZ), WIDE, 0,...  28.6 us
    all_to_all x2, waiting for transfers between devices, shared_by_all(): return lax.all_to_all(copies, axes, 0, 0, tiled=True)  24 us
    all_to_all x2, starting transfers between devices, shared_by_all(): return lax.all_to_all(copies, axes, 0, 0, tiled=True)  20.3 us
    all_to_all x1, local copies, waits for them, and re-layouts, local(): lax.all_to_all(slc.reshape(devices, columns // devices, 2, AZ), WIDE, 0,...  6.46 us
  transfers between devices with their start and end apart: 10, of which 8 were waited for; matrix products, arithmetic and copies ran while one was open for 6% of the time, Pallas kernels for 0%

commit v1 on v0

v1 whole, which is shorter than its diff:
```python
import math

import jax
import jax.numpy as jnp
from jax import lax
from jax.experimental import pallas as pl
from jax.experimental.pallas import tpu as pltpu
from jax.sharding import Mesh
from jax.sharding import PartitionSpec as P

AZ = 512
LOOK_AZ = 16
LOOK_RG = 16
LINE_CELLS = AZ // LOOK_AZ
WIDE = ("wide_0", "wide_1", "wide_2")
SLAB_WIDE = ("slab", "wide_0", "wide_1", "wide_2")
DAMPING = 1.0
DATES_STEP = 32
COLS_STEP = 8
CELLS_STEP = 8
ROT_ROWS = 16
LANES = 128
BLOCKS = AZ // LANES
COL_ROWS = 2 * BLOCKS
PACK_STEPS = 4


def spectral_table():
    ordinal = jnp.arange(AZ, dtype=jnp.int32)
    product = ordinal[:, None] * ordinal[None, :] % AZ
    angles = product.astype(jnp.float32) * (2.0 * math.pi / AZ)
    cosine = jnp.cos(angles).astype(jnp.bfloat16)
    sine = jnp.sin(angles).astype(jnp.bfloat16)
    return jnp.concatenate(
        [jnp.concatenate([cosine, -sine], 1), jnp.concatenate([sine, cosine], 1)], 0
    )


def pack_kernel(samples_ref, extra_ref, out_ref, buffer, extra_buffer, in_sem, out_sem):
    share = samples_ref.shape[0] // PACK_STEPS
    width = samples_ref.shape[1]
    rows = [pl.ds(i * share, share) for i in range(PACK_STEPS)]
    extra_in = pltpu.make_async_copy(extra_ref, extra_buffer, in_sem.at[PACK_STEPS])
    extra_out = pltpu.make_async_copy(
        extra_buffer, out_ref.at[:, pl.ds(width, 1)], out_sem.at[PACK_STEPS]
    )
    ins = [
        pltpu.make_async_copy(samples_ref.at[rows[i]], buffer.at[rows[i]], in_sem.at[i])
        for i in range(PACK_STEPS)
    ]
    outs = [
        pltpu.make_async_copy(
            buffer.at[rows[i]], out_ref.at[rows[i], pl.ds(0, width)], out_sem.at[i]
        )
        for i in range(PACK_STEPS)
    ]
    extra_in.start()
    for copy in ins:
        copy.start()
    extra_in.wait()
    extra_out.start()
    for copy_in, copy_out in zip(ins, outs):
        copy_in.wait()
        copy_out.start()
    extra_out.wait()
    for copy in outs:
        copy.wait()


def packed(samples, extra):
    devices, width = samples.shape[:2]
    return pl.pallas_call(
        pack_kernel,
        in_specs=[pl.BlockSpec(memory_space=pl.ANY)] * 2,
        out_specs=pl.BlockSpec(memory_space=pl.ANY),
        out_shape=jax.ShapeDtypeStruct((devices, width + 1, 2, LANES), samples.dtype),
        scratch_shapes=[
            pltpu.VMEM(samples.shape, samples.dtype),
            pltpu.VMEM(extra.shape, extra.dtype),
            pltpu.SemaphoreType.DMA((PACK_STEPS + 1,)),
            pltpu.SemaphoreType.DMA((PACK_STEPS + 1,)),
        ],
        name="pack",
    )(samples, extra)


def series(z):
    zz = z * z
    sin = z + z * zz * (
        -1.0 / 6 + zz * (1.0 / 120 + zz * (-1.0 / 5040 + zz * (1.0 / 362880)))
    )
    cos = 1.0 + zz * (
        -0.5 + zz * (1.0 / 24 + zz * (-1.0 / 720 + zz * (1.0 / 40320 + zz * (-1.0 / 3628800))))
    )
    return sin, cos


def turns(angle, lane):
    sin0, cos0 = series(angle * lane)
    sin_h, cos_h = series(angle * (LANES // 2))
    sin1, cos1 = 2.0 * sin_h * cos_h, 1.0 - 2.0 * sin_h * sin_h
    sin2, cos2 = 2.0 * sin1 * cos1, 1.0 - 2.0 * sin1 * sin1
    cc, ss, sc, cs = cos0 * cos1, sin0 * sin1, sin0 * cos1, cos0 * sin1
    return (
        (cos0, sin0),
        (cc - ss, sc + cs),
        (cos0 * cos2 + sin0 * sin2, sin0 * cos2 - cos0 * sin2),
        (cc + ss, sc - cs),
    )


def cells_kernel(
    x_ref, valid_ref, table_ref, second_ref, first_ref, coh_ref, ifg_ref, sums_ref,
    wide_ref, spec_ref, angle_ref, turned_ref, pix_ref, gamma_ref, int_ref,
):
    step = pl.program_id(0)
    dates = first_ref.shape[0]
    date_steps = dates // DATES_STEP
    range_steps = LOOK_RG // COLS_STEP
    stride = wide_ref.shape[0] // DATES_STEP

    @pl.when(step < date_steps)
    def _forward():
        wide_ref[...] = x_ref[...].astype(jnp.float32)
        valid = valid_ref[...]
        shifts = wide_ref[pl.ds(LOOK_RG * COL_ROWS, DATES_STEP, stride=stride), :]
        for c in range(LOOK_RG):
            parts = []
            for part in range(2):
                for block in range(BLOCKS):
                    rows = pl.ds(c * COL_ROWS + 2 * block + part, DATES_STEP, stride=stride)
                    parts.append(
                        (wide_ref[rows, :] * valid[:, block * LANES : (block + 1) * LANES]).astype(
                            jnp.bfloat16
                        )
                    )
            spec_ref[c * DATES_STEP : (c + 1) * DATES_STEP, :] = jnp.concatenate(parts, 1)
            angle_ref[c * DATES_STEP : (c + 1) * DATES_STEP, :] = jnp.broadcast_to(shifts[:, c : c + 1] * (
                -2.0 * math.pi / AZ
            ), (DATES_STEP, LANES))
        spec_ref[...] = jnp.dot(
            spec_ref[...], table_ref[...], preferred_element_type=jnp.float32
        ).astype(jnp.bfloat16)
        lane = lax.broadcasted_iota(jnp.int32, (1, LANES), 1).astype(jnp.float32)
        groups = DATES_STEP // ROT_ROWS

        def turn(i, _):
            rows = pl.ds(pl.multiple_of(i * ROT_ROWS, ROT_ROWS), ROT_ROWS)
            column, group = i // groups, i % groups
            target = pl.ds(
                pl.multiple_of(column * dates + step * DATES_STEP + group * ROT_ROWS, ROT_ROWS),
                ROT_ROWS,
            )
            for block, (cos, sin) in enumerate(turns(angle_ref[rows, :], lane)):
                at = slice(block * LANES, (block + 1) * LANES)
                at_imag = slice(AZ + block * LANES, AZ + (block + 1) * LANES)
                real = spec_ref[rows, at].astype(jnp.float32)
                imag = spec_ref[rows, at_imag].astype(jnp.float32)
                turned_ref[target, at] = (real * cos - imag * sin).astype(jnp.bfloat16)
                turned_ref[target, at_imag] = (real * sin + imag * cos).astype(jnp.bfloat16)
            return _

        lax.fori_loop(0, LOOK_RG * groups, turn, None)

    @pl.when((step >= date_steps) & (step < date_steps + range_steps))
    def _inverse():
        first_column = (step - date_steps) * COLS_STEP
        rows = pl.ds(pl.multiple_of(first_column * dates, COLS_STEP * dates), COLS_STEP * dates)
        restored = lax.dot_general(
            table_ref[...], turned_ref[rows, :], (((1,), (1,)), ((), ())),
            preferred_element_type=jnp.float32,
        )
        restored = (restored * (1.0 / AZ)).astype(jnp.bfloat16)
        for c in range(COLS_STEP):
            pix_ref[:, :, first_column + c] = restored[:, c * dates : (c + 1) * dates].reshape(
                2, LINE_CELLS, LOOK_AZ, dates
            )

    @pl.when(step >= date_steps + range_steps)
    def _covariance():
        diagonal = lax.broadcasted_iota(jnp.int32, (dates, dates), 0) == lax.broadcasted_iota(
            jnp.int32, (dates, dates), 1
        )
        base = (step - date_steps - range_steps) * CELLS_STEP
        for k in range(CELLS_STEP):
            real = pix_ref[0, base + k].reshape(LOOK_RG * LOOK_AZ, dates)
            imag = pix_ref[1, base + k].reshape(LOOK_RG * LOOK_AZ, dates)
            pixels = jnp.concatenate([real, imag], 0)
            partner = jnp.concatenate([pixels, jnp.concatenate([-imag, real], 0)], 1)
            cov = lax.dot_general(
                pixels, partner, (((0,), (0,)), ((), ())), preferred_element_type=jnp.float32
            )
            on_diagonal = jnp.where(diagonal, cov[:, :dates], 0.0)
            scale_rows = lax.rsqrt(jnp.sum(on_diagonal, 1, keepdims=True) + DAMPING)
            scale_cols = lax.rsqrt(jnp.sum(on_diagonal, 0, keepdims=True) + DAMPING)
            scale = scale_rows * scale_cols
            for part in range(2):
                gamma = cov[:, part * dates : (part + 1) * dates] * scale
                high = gamma.astype(jnp.bfloat16)
                coh_ref[k, part] = high
                rows = slice((2 * k + part) * dates, (2 * k + part + 1) * dates)
                gamma_ref[rows, :dates] = high
                gamma_ref[rows, dates:] = (gamma - high.astype(jnp.float32)).astype(jnp.bfloat16)
        picked = jnp.dot(gamma_ref[...], second_ref[...], preferred_element_type=jnp.float32)
        first = first_ref[...]
        for k in range(CELLS_STEP):
            for part in range(2):
                rows = slice((2 * k + part) * dates, (2 * k + part + 1) * dates)
                int_ref[base + k, part : part + 1, :] = jnp.sum(
                    picked[rows] * first, 0, keepdims=True
                )

    @pl.when(step == pl.num_programs(0) - 1)
    def _sums():
        ifg = int_ref[...]
        ifg_ref[...] = ifg
        real, imag = ifg[:, 0, :], ifg[:, 1, :]
        weight = 0.1 + real * real + imag * imag
        line = lax.broadcasted_iota(jnp.int32, (LINE_CELLS, 1), 0).astype(jnp.float32)
        across = (line + 0.5) / LINE_CELLS - 0.5
        tilted = weight * across
        terms = (
            weight, tilted, tilted * across, weight * real, tilted * real, weight * imag, tilted * imag
        )
        for k, term in enumerate(terms):
            sums_ref[k : k + 1, :] = jnp.sum(term, 0, keepdims=True)
        sums_ref[len(terms) :, :] = jnp.zeros_like(sums_ref[len(terms) :, :])


def cells_call(x, valid, table, second, first):
    dates, pairs = first.shape
    date_steps = dates // DATES_STEP
    before = date_steps + LOOK_RG // COLS_STEP
    steps = before + LINE_CELLS // CELLS_STEP
    stride = x.shape[0] // dates
    last = date_steps - 1

    def whole(*shape):
        return pl.BlockSpec(shape, lambda s: (0,) * len(shape))

    return pl.pallas_call(
        cells_kernel,
        grid=(steps,),
        in_specs=[
            pl.BlockSpec((DATES_STEP * stride, LANES), lambda s: (jnp.minimum(s, last), 0)),
            pl.BlockSpec((DATES_STEP, AZ), lambda s: (jnp.minimum(s, last), 0)),
            whole(2 * AZ, 2 * AZ),
            whole(2 * dates, pairs),
            whole(dates, pairs),
        ],
        out_specs=[
            pl.BlockSpec(
                (CELLS_STEP, 2, dates, dates), lambda s: (jnp.maximum(s - before, 0), 0, 0, 0)
            ),
            whole(LINE_CELLS, 2, pairs),
            whole(8, pairs),
        ],
        out_shape=[
            jax.ShapeDtypeStruct((LINE_CELLS, 2, dates, dates), jnp.bfloat16),
            jax.ShapeDtypeStruct((LINE_CELLS, 2, pairs), jnp.float32),
            jax.ShapeDtypeStruct((8, pairs), jnp.float32),
        ],
        scratch_shapes=[
            pltpu.VMEM((DATES_STEP * stride, LANES), jnp.float32),
            pltpu.VMEM((LOOK_RG * DATES_STEP, 2 * AZ), jnp.bfloat16),
            pltpu.VMEM((LOOK_RG * DATES_STEP, LANES), jnp.float32),
            pltpu.VMEM((LOOK_RG * dates, 2 * AZ), jnp.bfloat16),
            pltpu.VMEM((2, LINE_CELLS, LOOK_RG, LOOK_AZ, dates), jnp.bfloat16),
            pltpu.VMEM((2 * CELLS_STEP * dates, 2 * dates), jnp.bfloat16),
            pltpu.VMEM((LINE_CELLS, 2, pairs), jnp.float32),
        ],
        compiler_params=pltpu.CompilerParams(dimension_semantics=("arbitrary",)),
        name="cells",
    )(x, valid, table, second, first)


def line_blocks(samples):
    count, columns = samples.shape[:2]
    blocks = samples.reshape(count, columns, 2, BLOCKS, LANES).transpose(0, 1, 3, 2, 4)
    return blocks.reshape(count, columns * BLOCKS, 2, LANES)


def plane_terms(sums, along):
    w0, w1, w2, r0, r1, i0, i1 = (sums[k] for k in range(7))
    terms = (
        w0, w1, w0 * along, w2, w1 * along, w0 * along * along,
        r0, r1, r0 * along, i0, i1, i0 * along,
    )
    return jnp.stack(terms, 0)


def solve_three(n):
    adjugate_00 = n[3] * n[5] - n[4] * n[4]
    adjugate_01 = n[2] * n[4] - n[1] * n[5]
    adjugate_02 = n[1] * n[4] - n[2] * n[3]
    adjugate_11 = n[0] * n[5] - n[2] * n[2]
    adjugate_12 = n[1] * n[2] - n[0] * n[4]
    adjugate_22 = n[0] * n[3] - n[1] * n[1]
    determinant = n[0] * adjugate_00 + n[1] * adjugate_01 + n[2] * adjugate_02
    parts = []
    for t in (n[6:9], n[9:12]):
        parts.append(
            jnp.stack(
                [
                    adjugate_00 * t[0] + adjugate_01 * t[1] + adjugate_02 * t[2],
                    adjugate_01 * t[0] + adjugate_11 * t[1] + adjugate_12 * t[2],
                    adjugate_02 * t[0] + adjugate_12 * t[1] + adjugate_22 * t[2],
                ],
                0,
            )
            / determinant
        )
    return jnp.stack(parts, 0)


def summed_over(array, axis):
    copies = jnp.broadcast_to(array[None], (lax.axis_size(axis), *array.shape))
    return jnp.sum(lax.all_to_all(copies, axis, 0, 0, tiled=True), 0)


def along_of(position, range_cells):
    return (position.astype(jnp.float32) + 0.5) / range_cells - 0.5


def fitted(sums, range_cells):
    core = lax.axis_index("wide_2")
    position = lax.axis_index(WIDE)
    other = position + 1 - 2 * core
    swap = [(0, 1), (1, 0)]
    halves = sums.reshape(sums.shape[0], 2, -1)
    keep = jnp.where(core == 0, halves[:, 0], halves[:, 1])
    give = jnp.where(core == 0, halves[:, 1], halves[:, 0])
    got = lax.ppermute(give, "wide_2", swap)
    terms = plane_terms(keep, along_of(position, range_cells)) + plane_terms(
        got, along_of(other, range_cells)
    )
    ramps = solve_three(summed_over(summed_over(terms, "wide_1"), "wide_0"))
    others = lax.ppermute(ramps, "wide_2", swap)
    return jnp.where(
        core == 0, jnp.concatenate([ramps, others], -1), jnp.concatenate([others, ramps], -1)
    )


def local(slc, offsets, row_start, row_stop, pairs):
    devices = lax.axis_size(WIDE)
    position = lax.axis_index(WIDE)
    columns = slc.shape[1]
    here = columns // devices
    dates = devices * slc.shape[0]
    extra = jnp.pad(offsets.reshape(devices, 1, 1, here), ((0, 0), (0, 0), (0, 1), (0, LANES - here)))
    sent = packed(line_blocks(slc.reshape(devices, here, 2, AZ)), extra)
    received = lax.all_to_all(sent, WIDE, 0, 0, tiled=True)
    lines = jnp.arange(AZ, dtype=jnp.int32)[None, :]
    valid = ((lines >= row_start[:, None]) & (lines < row_stop[:, None])).astype(jnp.float32)
    date = jnp.arange(dates, dtype=jnp.int32)[:, None]
    first = (date == pairs[:, 0][None, :]).astype(jnp.float32)
    second = (date == pairs[:, 1][None, :]).astype(jnp.bfloat16)
    second = jnp.concatenate([second, second], 0)
    coherence, ifg, sums = cells_call(
        received.reshape(-1, LANES), valid, spectral_table(), second, first
    )

    range_cells = columns // LOOK_RG
    ramps = fitted(sums, range_cells)
    share = pairs.shape[0] // devices
    own = lax.dynamic_slice_in_dim(ramps, position * share, share, 2).transpose(2, 0, 1)
    across = (jnp.arange(LINE_CELLS, dtype=jnp.int32).astype(jnp.float32) + 0.5) / LINE_CELLS - 0.5
    along = along_of(position, range_cells)
    plane = ramps[:, 0] + across[:, None, None] * ramps[:, 1] + along * ramps[:, 2]
    return coherence, ifg - plane, own


def solution(mesh):
    torus = Mesh(
        mesh.devices.reshape(mesh.shape["slab"], 8, 8, 2), ("slab", "wide_0", "wide_1", "wide_2")
    )
    in_specs = (P(WIDE, "slab", None, None), P(WIDE, "slab"), P(), P(), P())
    out_specs = (P(SLAB_WIDE, None, None, None), P(SLAB_WIDE, None, None), P(SLAB_WIDE, None, None))
    return jax.shard_map(local, mesh=torus, in_specs=in_specs, out_specs=out_specs, check_vma=False)
```

time: 251 us -> 199 us (0.79)
  the two profiles are of different devices: /device:TPU:513 before, /device:TPU:641 now
where the time goes in v1:
time: 199 us
  waiting for transfers between devices  87 us (44%)
  blocking collectives  40.2 us (20%)
  starting transfers between devices  27.7 us (14%)
  Pallas kernels  26.7 us (13%)
  other arithmetic  14.9 us (7%)
    all_to_all x1, waiting for transfers between devices, local(): received = lax.all_to_all(sent, WIDE, 0, 0, tiled=True)  85.4 us
    all_to_all x2, blocking collectives, summed_over(): return jnp.sum(lax.all_to_all(copies, axis, 0, 0, tiled=True), 0)  40.2 us
    pallas_call x1, Pallas kernels, cells_call(): pl.pallas_call(cells_kernel, grid=(steps,), in_specs=[pl.BlockSpec((DATES...  23.2 us
    all_to_all x1, starting transfers between devices, local(): received = lax.all_to_all(sent, WIDE, 0, 0, tiled=True)  22.5 us
    convert_element_type x1, other arithmetic, spectral_table(): sine = jnp.sin(angles).astype(jnp.bfloat16)  4.31 us
    neg x1, other arithmetic, spectral_table(): -sine  3.99 us
  transfers between devices with their start and end apart: 3, of which 3 were waited for; matrix products, arithmetic and copies ran while one was open for 6% of the time, Pallas kernels for 0%

profile of v1, /device:TPU:641, one launch (start us, length us, event | category | flops | bytes accessed | tf_op | source)
XLA Modules:
  0.0 199.0 jit_solution(243523456635066260)
XLA Ops:
  0.6 0.7 reduce
  1.4 0.1 reshape.322
  1.5 0.7 pad.4.extra_ref
  2.2 3.5 %pack.1 = bf16[128,65,2,128]{3,2,1,0:T(2,128)(2,1)} custom-call(bf16[128,64,2,128]{3,2,1,0:T(2,128)(2,1)} %bitcast.50, bf16[128,1,2,128]{3,2,1,0:T(2,128)(2,1)} %pad.4.extra_ref), custom_call_target="tpu_custom_call" | custom-call | tf_op jit(solution)/shard_map/pack/pallas_call | solution.py:72
  5.6 0.0 copy-start
  5.7 22.5 %all-to-all-start = ((bf16[128,65,2,128]{3,2,1,0:T(2,128)(2,1)}), bf16[128,65,2,128]{3,2,1,0:T(2,128)(2,1)}, u32[]{:S(2)}, u32[]{:S(2)}) async-start(bf16[128,65,2,128]{3,2,1,0:T(2,128)(2,1)} %pack.1), calls=%async_computation | async-start | bytes 8519680 | tf_op jit(solution)/shard_map/all_to_all | solution.py:352
  28.1 0.0 copy-start.1
  28.2 0.0 copy-start.2
  28.2 0.0 copy-done
  28.3 0.7 add_convert_fusion.second_ref
  29.0 4.0 %fusion.9 = bf16[512,512]{1,0:T(8,128)(2,1)S(1)} fusion(), kind=kLoop, calls=%fused_computation.20 | loop fusion | flops 4718592 | bytes 524288 | tf_op jit(solution)/shard_map/neg | solution.py:35
  33.0 4.3 %sine_convert_fusion = (bf16[512,512]{1,0:T(8,128)(2,1)S(1)}, bf16[512,512]{1,0:T(8,128)(2,1)S(1)}) fusion(), kind=kLoop, calls=%fused_computation.7 | loop fusion | flops 4194304 | bytes 1048576 | tf_op jit(solution)/shard_map/convert_element_type | solution.py:33
  37.3 1.7 maximum_maximum_fusion.table_ref
  39.0 0.0 copy-done.1
  39.0 0.0 copy-done.2
  39.0 0.8 fusion.7
  39.9 85.4 %all-to-all-done = bf16[128,65,2,128]{3,2,1,0:T(2,128)(2,1)} async-done(((bf16[128,65,2,128]{3,2,1,0:T(2,128)(2,1)}), bf16[128,65,2,128]{3,2,1,0:T(2,128)(2,1)}, u32[]{:S(2)}, u32[]{:S(2)}) %all-to-all-start) | async-done | bytes 4259872 | tf_op jit(solution)/shard_map/all_to_all | solution.py:352
  125.3 23.2 %cells.1 = (bf16[32,2,128,128]{3,2,1,0:T(8,128)(2,1)}, f32[32,2,512]{2,1,0:T(2,128)}, f32[8,512]{1,0:T(8,128)}) custom-call(bf16[16640,128]{1,0:T(8,128)(2,1)} %bitcast.3.x_ref, f32[128,512]{1,0:T(8,128)} %get-tuple-element.46.valid_ref, bf16[1024,1024]{1,0:T(8,128)(2,1)} %maximum_maximum_fusion.table_ref, bf16[256,512]{1,0:T(8,128)(2,1)} %add_convert_fusion.second_ref, ...), custom_call_target="tpu_custom_call" | custom-call | tf_op jit(solution)/shard_map/cells/pallas_call | solution.py:241
  148.5 0.7 select_bitcast_fusion
  149.2 1.7 collective-permute-start
  151.0 0.8 collective-permute-done
  151.8 12.2 %all_to_all.15 = f32[8,12,256]{2,1,0:T(8,128)S(1)} all-to-all(f32[8,12,256]{2,1,0:T(8,128)S(1)} %broadcast_in_dim.4), channel_id=1, replica_groups=mesh['slab'=2,'wide_0'=8,'wide_1'=8,'wide_2'=2] {'wide_1'}, dimensions={0} | all-to-all | bytes 196608 | tf_op jit(solution)/shard_map/all_to_all | solution.py:318
  164.0 28.0 %all_to_all.16 = f32[8,12,256]{2,1,0:T(8,128)S(1)} all-to-all(f32[8,12,256]{2,1,0:T(8,128)S(1)} %broadcast_in_dim.5), channel_id=1, replica_groups=mesh['slab'=2,'wide_0'=8,'wide_1'=8,'wide_2'=2] {'wide_0'}, dimensions={0} | all-to-all | bytes 196608 | tf_op jit(solution)/shard_map/all_to_all | solution.py:318
  192.2 3.5 %collective-permute-start.1 = (f32[2,3,256]{2,0,1:T(2,128)S(1)}, f32[2,3,256]{2,0,1:T(2,128)S(1)}, u32[]{:S(2)}, u32[]{:S(2)}) collective-permute-start(f32[2,3,256]{2,0,1:T(2,128)S(1)} %pad_maximum_fusion), channel_id=1, source_target_pairs={{0,1},{1,0},{2,3},{3,2},{4,5},{5,4},{6,7},{7,6},{8,9},{9,8},{10,11... | collective-permute-start | bytes 18440 | tf_op jit(solution)/shard_map/ppermute | solution.py:338
  195.7 0.8 collective-permute-done.1
  196.6 0.7 dynamic-slice_bitcast_fusion
  197.3 1.7 add_subtract_fusion
  (24 shorter events, 0.3 us)
Async XLA Ops:
  5.6 22.5 %copy-start = (s32[512,2]{0,1:T(2,128)S(1)}, s32[512,2]{0,1:T(2,128)}, u32[]{:S(2)}) copy-start(s32[512,2]{0,1:T(2,128)} %param.9) | copy-start | bytes 12292
  5.7 119.6 %all-to-all-start = ((bf16[128,65,2,128]{3,2,1,0:T(2,128)(2,1)}), bf16[128,65,2,128]{3,2,1,0:T(2,128)(2,1)}, u32[]{:S(2)}, u32[]{:S(2)}) async-start(bf16[128,65,2,128]{3,2,1,0:T(2,128)(2,1)} %pack.1), calls=%async_computation | async-start | bytes 8519680 | tf_op jit(solution)/shard_map/all_to_all | solution.py:352
  28.1 10.9 %copy-start.1 = (s32[128]{0:T(128)S(1)}, s32[128]{0:T(128)}, u32[]{:S(2)}) copy-start(s32[128]{0:T(128)} %param.8) | copy-start | bytes 1540
  28.2 10.9 %copy-start.2 = (s32[128]{0:T(128)S(1)}, s32[128]{0:T(128)}, u32[]{:S(2)}) copy-start(s32[128]{0:T(128)} %param.7) | copy-start | bytes 1540
  149.2 2.5 %collective-permute-start = (f32[8,256]{1,0:T(8,128)S(1)}, f32[8,256]{1,0:T(8,128)S(1)}, u32[]{:S(2)}, u32[]{:S(2)}) collective-permute-start(f32[8,256]{1,0:T(8,128)S(1)} %get-tuple-element.18), channel_id=1, source_target_pairs={{0,1},{1,0},{2,3},{3,2},{4,5},{5,4},{6,7},{7,6},{8,9},{9,8},{10,11... | collective-permute-start | bytes 24584 | tf_op jit(solution)/shard_map/ppermute | solution.py:333
  192.2 4.4 %collective-permute-start.1 = (f32[2,3,256]{2,0,1:T(2,128)S(1)}, f32[2,3,256]{2,0,1:T(2,128)S(1)}, u32[]{:S(2)}, u32[]{:S(2)}) collective-permute-start(f32[2,3,256]{2,0,1:T(2,128)S(1)} %pad_maximum_fusion), channel_id=1, source_target_pairs={{0,1},{1,0},{2,3},{3,2},{4,5},{5,4},{6,7},{7,6},{8,9},{9,8},{10,11... | collective-permute-start | bytes 18440 | tf_op jit(solution)/shard_map/ppermute | solution.py:338

commit v2 on v1

--- a/solution.py
+++ b/solution.py
@@ -18,32 +18,38 @@
 DATES_STEP = 32
 COLS_STEP = 8
 CELLS_STEP = 8
-ROT_ROWS = 16
+ROT_ROWS = 32
 LANES = 128
 BLOCKS = AZ // LANES
+HALF = AZ // 2
 COL_ROWS = 2 * BLOCKS
 PACK_STEPS = 4
 
 
-def spectral_table():
-    ordinal = jnp.arange(AZ, dtype=jnp.int32)
-    product = ordinal[:, None] * ordinal[None, :] % AZ
-    angles = product.astype(jnp.float32) * (2.0 * math.pi / AZ)
-    cosine = jnp.cos(angles).astype(jnp.bfloat16)
-    sine = jnp.sin(angles).astype(jnp.bfloat16)
-    return jnp.concatenate(
-        [jnp.concatenate([cosine, -sine], 1), jnp.concatenate([sine, cosine], 1)], 0
-    )
-
-
-def pack_kernel(samples_ref, extra_ref, out_ref, buffer, extra_buffer, in_sem, out_sem):
-    share = samples_ref.shape[0] // PACK_STEPS
-    width = samples_ref.shape[1]
+def bins_of(odd):
+    j = 2 * jnp.arange(HALF // 2, dtype=jnp.int32) + odd
+    return jnp.concatenate([j, jnp.where(j == 0, AZ // 2, AZ - j)], 0)
+
+
+def spectral_tables():
+    line = jnp.arange(HALF, dtype=jnp.int32)[:, None]
+    tables = []
+    for odd in range(2):
+        angles = (line * bins_of(odd)[None, :] % AZ).astype(jnp.float32) * (2.0 * math.pi / AZ)
+        cosine = jnp.cos(angles).astype(jnp.bfloat16)
+        sine = jnp.sin(angles).astype(jnp.bfloat16)
+        tables.append(
+            jnp.concatenate(
+                [jnp.concatenate([cosine, -sine], 1), jnp.concatenate([sine, cosine], 1)], 0
+            )
+        )
+    return jnp.stack(tables, 0)
+
+
+def pack_kernel(samples_ref, offsets_ref, out_ref, buffer, own, extra_buffer, in_sem, out_sem):
+    devices, width = samples_ref.shape[:2]
+    share = devices // PACK_STEPS
     rows = [pl.ds(i * share, share) for i in range(PACK_STEPS)]
-    extra_in = pltpu.make_async_copy(extra_ref, extra_buffer, in_sem.at[PACK_STEPS])
-    extra_out = pltpu.make_async_copy(
-        extra_buffer, out_ref.at[:, pl.ds(width, 1)], out_sem.at[PACK_STEPS]
-    )
     ins = [
         pltpu.make_async_copy(samples_ref.at[rows[i]], buffer.at[rows[i]], in_sem.at[i])
         for i in range(PACK_STEPS)
@@ -54,20 +60,29 @@
         )
         for i in range(PACK_STEPS)
     ]
-    extra_in.start()
+    own_in = pltpu.make_async_copy(offsets_ref, own, in_sem.at[PACK_STEPS])
+    own_in.start()
     for copy in ins:
         copy.start()
-    extra_in.wait()
-    extra_out.start()
+    own_in.wait()
+    sharing = devices * LANES // offsets_ref.shape[1]
+    for k in range(devices // sharing):
+        block = jnp.broadcast_to(own[:, k * LANES : (k + 1) * LANES], (2, LANES))
+        for i in range(sharing):
+            extra_buffer[k * sharing + i, 0] = block
+    extra = pltpu.make_async_copy(
+        extra_buffer, out_ref.at[:, pl.ds(width, 1)], out_sem.at[PACK_STEPS]
+    )
+    extra.start()
     for copy_in, copy_out in zip(ins, outs):
         copy_in.wait()
         copy_out.start()
-    extra_out.wait()
+    extra.wait()
     for copy in outs:
         copy.wait()
 
 
-def packed(samples, extra):
+def packed(samples, offsets):
     devices, width = samples.shape[:2]
     return pl.pallas_call(
         pack_kernel,
@@ -76,12 +91,13 @@
         out_shape=jax.ShapeDtypeStruct((devices, width + 1, 2, LANES), samples.dtype),
         scratch_shapes=[
             pltpu.VMEM(samples.shape, samples.dtype),
-            pltpu.VMEM(extra.shape, extra.dtype),
+            pltpu.VMEM(offsets.shape, offsets.dtype),
+            pltpu.VMEM((devices, 1, 2, LANES), samples.dtype),
             pltpu.SemaphoreType.DMA((PACK_STEPS + 1,)),
             pltpu.SemaphoreType.DMA((PACK_STEPS + 1,)),
         ],
         name="pack",
-    )(samples, extra)
+    )(samples, offsets)
 
 
 def series(z):
@@ -92,25 +108,22 @@
     cos = 1.0 + zz * (
         -0.5 + zz * (1.0 / 24 + zz * (-1.0 / 720 + zz * (1.0 / 40320 + zz * (-1.0 / 3628800))))
     )
-    return sin, cos
+    return cos, sin
 
 
 def turns(angle, lane):
-    sin0, cos0 = series(angle * lane)
-    sin_h, cos_h = series(angle * (LANES // 2))
-    sin1, cos1 = 2.0 * sin_h * cos_h, 1.0 - 2.0 * sin_h * sin_h
-    sin2, cos2 = 2.0 * sin1 * cos1, 1.0 - 2.0 * sin1 * sin1
-    cc, ss, sc, cs = cos0 * cos1, sin0 * sin1, sin0 * cos1, cos0 * sin1
-    return (
-        (cos0, sin0),
-        (cc - ss, sc + cs),
-        (cos0 * cos2 + sin0 * sin2, sin0 * cos2 - cos0 * sin2),
-        (cc + ss, sc - cs),
-    )
+    cos, sin = series(angle * jnp.where(lane == 0.0, HALF / 2.0, lane))
+    cos, sin = 1.0 - 2.0 * sin * sin, 2.0 * sin * cos
+    even_cos, even_sin = jnp.where(lane == 0.0, 1.0, cos), jnp.where(lane == 0.0, 0.0, sin)
+    square = angle * angle
+    one_cos, one_sin = 1.0 - square * (0.5 - square * (1.0 / 24)), angle - angle * square * (1.0 / 6)
+    odd_cos = even_cos * one_cos - even_sin * one_sin
+    odd_sin = even_cos * one_sin + even_sin * one_cos
+    return (even_cos, even_sin), (cos, -sin), (odd_cos, odd_sin), (odd_cos, -odd_sin)
 
 
 def cells_kernel(
-    x_ref, valid_ref, table_ref, second_ref, first_ref, coh_ref, ifg_ref, sums_ref,
+    at_ref, x_ref, valid_ref, table_ref, second_ref, first_ref, coh_ref, ifg_ref, sums_ref,
     wide_ref, spec_ref, angle_ref, turned_ref, pix_ref, gamma_ref, int_ref,
 ):
     step = pl.program_id(0)
@@ -124,23 +137,28 @@
         wide_ref[...] = x_ref[...].astype(jnp.float32)
         valid = valid_ref[...]
         shifts = wide_ref[pl.ds(LOOK_RG * COL_ROWS, DATES_STEP, stride=stride), :]
+        shifts = pltpu.roll(shifts, at_ref[0], 1)
         for c in range(LOOK_RG):
-            parts = []
+            sums, differences = [], []
             for part in range(2):
-                for block in range(BLOCKS):
-                    rows = pl.ds(c * COL_ROWS + 2 * block + part, DATES_STEP, stride=stride)
-                    parts.append(
-                        (wide_ref[rows, :] * valid[:, block * LANES : (block + 1) * LANES]).astype(
-                            jnp.bfloat16
-                        )
+                for block in range(BLOCKS // 2):
+                    low, high = (
+                        wide_ref[pl.ds(c * COL_ROWS + 2 * b + part, DATES_STEP, stride=stride), :]
+                        * valid[:, b * LANES : (b + 1) * LANES]
+                        for b in (block, block + BLOCKS // 2)
                     )
-            spec_ref[c * DATES_STEP : (c + 1) * DATES_STEP, :] = jnp.concatenate(parts, 1)
-            angle_ref[c * DATES_STEP : (c + 1) * DATES_STEP, :] = jnp.broadcast_to(shifts[:, c : c + 1] * (
-                -2.0 * math.pi / AZ
-            ), (DATES_STEP, LANES))
-        spec_ref[...] = jnp.dot(
-            spec_ref[...], table_ref[...], preferred_element_type=jnp.float32
-        ).astype(jnp.bfloat16)
+                    sums.append((low + high).astype(jnp.bfloat16))
+                    differences.append((low - high).astype(jnp.bfloat16))
+            rows = slice(c * DATES_STEP, (c + 1) * DATES_STEP)
+            spec_ref[rows, :] = jnp.concatenate(sums + differences, 1)
+            angle_ref[rows, :] = jnp.broadcast_to(
+                shifts[:, c : c + 1] * (-2.0 * math.pi / AZ), (DATES_STEP, LANES)
+            )
+        for odd in range(2):
+            at = slice(odd * AZ, (odd + 1) * AZ)
+            spec_ref[:, at] = jnp.dot(
+                spec_ref[:, at], table_ref[odd], preferred_element_type=jnp.float32
+            ).astype(jnp.bfloat16)
         lane = lax.broadcasted_iota(jnp.int32, (1, LANES), 1).astype(jnp.float32)
         groups = DATES_STEP // ROT_ROWS
 
@@ -152,8 +170,8 @@
                 ROT_ROWS,
             )
             for block, (cos, sin) in enumerate(turns(angle_ref[rows, :], lane)):
-                at = slice(block * LANES, (block + 1) * LANES)
-                at_imag = slice(AZ + block * LANES, AZ + (block + 1) * LANES)
+                start = (block // 2) * AZ + (block % 2) * LANES
+                at, at_imag = slice(start, start + LANES), slice(start + HALF, start + HALF + LANES)
                 real = spec_ref[rows, at].astype(jnp.float32)
                 imag = spec_ref[rows, at_imag].astype(jnp.float32)
                 turned_ref[target, at] = (real * cos - imag * sin).astype(jnp.bfloat16)
@@ -166,15 +184,20 @@
     def _inverse():
         first_column = (step - date_steps) * COLS_STEP
         rows = pl.ds(pl.multiple_of(first_column * dates, COLS_STEP * dates), COLS_STEP * dates)
-        restored = lax.dot_general(
-            table_ref[...], turned_ref[rows, :], (((1,), (1,)), ((), ())),
-            preferred_element_type=jnp.float32,
-        )
-        restored = (restored * (1.0 / AZ)).astype(jnp.bfloat16)
-        for c in range(COLS_STEP):
-            pix_ref[:, :, first_column + c] = restored[:, c * dates : (c + 1) * dates].reshape(
-                2, LINE_CELLS, LOOK_AZ, dates
-            )
+        even, odd = (
+            lax.dot_general(
+                table_ref[k], turned_ref[rows, k * AZ : (k + 1) * AZ], (((1,), (1,)), ((), ())),
+                preferred_element_type=jnp.float32,
+            )
+            for k in range(2)
+        )
+        for half, restored in enumerate((even + odd, even - odd)):
+            restored = (restored * (1.0 / AZ)).astype(jnp.bfloat16)
+            cells = slice(half * LINE_CELLS // 2, (half + 1) * LINE_CELLS // 2)
+            for c in range(COLS_STEP):
+                pix_ref[:, cells, first_column + c] = restored[
+                    :, c * dates : (c + 1) * dates
+                ].reshape(2, LINE_CELLS // 2, LOOK_AZ, dates)
 
     @pl.when(step >= date_steps + range_steps)
     def _covariance():
@@ -227,7 +250,7 @@
         sums_ref[len(terms) :, :] = jnp.zeros_like(sums_ref[len(terms) :, :])
 
 
-def cells_call(x, valid, table, second, first):
+def cells_call(at, x, valid, table, second, first):
     dates, pairs = first.shape
     date_steps = dates // DATES_STEP
     before = date_steps + LOOK_RG // COLS_STEP
@@ -242,11 +265,12 @@
         cells_kernel,
         grid=(steps,),
         in_specs=[
+            pl.BlockSpec(memory_space=pltpu.SMEM),
             pl.BlockSpec((DATES_STEP * stride, LANES), lambda s: (jnp.minimum(s, last), 0)),
             pl.BlockSpec((DATES_STEP, AZ), lambda s: (jnp.minimum(s, last), 0)),
-            whole(2 * AZ, 2 * AZ),
-            whole(2 * dates, pairs),
-            whole(dates, pairs),
+            pl.BlockSpec(memory_space=pltpu.VMEM),
+            pl.BlockSpec(memory_space=pltpu.VMEM),
+            pl.BlockSpec(memory_space=pltpu.VMEM),
         ],
         out_specs=[
             pl.BlockSpec(
@@ -269,9 +293,11 @@
             pltpu.VMEM((2 * CELLS_STEP * dates, 2 * dates), jnp.bfloat16),
             pltpu.VMEM((LINE_CELLS, 2, pairs), jnp.float32),
         ],
-        compiler_params=pltpu.CompilerParams(dimension_semantics=("arbitrary",)),
+        compiler_params=pltpu.CompilerParams(
+            dimension_semantics=("arbitrary",), vmem_limit_bytes=48 * 1024 * 1024
+        ),
         name="cells",
-    )(x, valid, table, second, first)
+    )(at, x, valid, table, second, first)
 
 
 def line_blocks(samples):
@@ -347,8 +373,8 @@
     columns = slc.shape[1]
     here = columns // devices
     dates = devices * slc.shape[0]
-    extra = jnp.pad(offsets.reshape(devices, 1, 1, here), ((0, 0), (0, 0), (0, 1), (0, LANES - here)))
-    sent = packed(line_blocks(slc.reshape(devices, here, 2, AZ)), extra)
+    at = (LANES - here * (position % (LANES // here))) % LANES
+    sent = packed(line_blocks(slc.reshape(devices, here, 2, AZ)), offsets)
     received = lax.all_to_all(sent, WIDE, 0, 0, tiled=True)
     lines = jnp.arange(AZ, dtype=jnp.int32)[None, :]
     valid = ((lines >= row_start[:, None]) & (lines < row_stop[:, None])).astype(jnp.float32)
@@ -357,7 +383,7 @@
     second = (date == pairs[:, 1][None, :]).astype(jnp.bfloat16)
     second = jnp.concatenate([second, second], 0)
     coherence, ifg, sums = cells_call(
-        received.reshape(-1, LANES), valid, spectral_table(), second, first
+        at.reshape(1), received.reshape(-1, LANES), valid, spectral_tables(), second, first
     )
 
     range_cells = columns // LOOK_RG

time: 199 us -> 189 us (0.950)
  other arithmetic: 14.9 us -> 5.57 us
  waiting for transfers between devices: 87 us -> 95.3 us
  Pallas kernels: 26.7 us -> 20.5 us
    all_to_all x1, waiting for transfers between devices: 85.4 us -> 93.6 us  [local(): received = lax.all_to_all(sent, WIDE, 0, 0, tiled=True)]
    pallas_call x1, Pallas kernels: 23.2 us -> 17 us  [cells_call(): pl.pallas_call(cells_kernel, grid=(steps,), in_specs=[pl.BlockSpec(memory...]
    convert_element_type x1 -> x2, other arithmetic: 4.31 us -> 2.24 us  [spectral_tables(): sine = jnp.sin(angles).astype(jnp.bfloat16)]
    neg x1 -> x2, other arithmetic: 3.99 us -> 1.98 us  [spectral_tables(): -sine]
  transfers between devices with their start and end apart: 3 -> 3, of which waited for: 3 -> 3; matrix products, arithmetic and copies ran while one was open for 6% -> 2% of each run, Pallas kernels for 0% -> 0%
where the time goes in v2:
time: 189 us; the launch traced here: 188 us
  waiting for transfers between devices  95.3 us (50%)
  blocking collectives  38.7 us (20%)
  starting transfers between devices  26.4 us (14%)
  Pallas kernels  20.5 us (11%)
  other arithmetic  5.57 us (3%)
    all_to_all x1, waiting for transfers between devices, local(): received = lax.all_to_all(sent, WIDE, 0, 0, tiled=True)  93.6 us
    all_to_all x2, blocking collectives, summed_over(): return jnp.sum(lax.all_to_all(copies, axis, 0, 0, tiled=True), 0)  38.7 us
    all_to_all x1, starting transfers between devices, local(): received = lax.all_to_all(sent, WIDE, 0, 0, tiled=True)  22.5 us
    pallas_call x1, Pallas kernels, cells_call(): pl.pallas_call(cells_kernel, grid=(steps,), in_specs=[pl.BlockSpec(memory...  17 us
  transfers between devices with their start and end apart: 3, of which 3 were waited for; matrix products, arithmetic and copies ran while one was open for 2% of the time, Pallas kernels for 0%

profile of v2, /device:TPU:641, one launch (start us, length us, event | category | flops | bytes accessed | tf_op | source)
XLA Modules:
  0.0 188.2 jit_solution(6172364267729210417)
XLA Ops:
  0.6 3.5 %pack.1 = bf16[128,65,2,128]{3,2,1,0:T(2,128)(2,1)} custom-call(bf16[128,64,2,128]{3,2,1,0:T(2,128)(2,1)} %bitcast.56, bf16[1,2048]{1,0:T(2,128)(2,1)} %offsets_ref.1), custom_call_target="tpu_custom_call" | custom-call | tf_op jit(solution)/shard_map/pack/pallas_call | solution.py:87
  4.1 0.0 copy-start
  4.1 22.5 %all-to-all-start = ((bf16[128,65,2,128]{3,2,1,0:T(2,128)(2,1)}), bf16[128,65,2,128]{3,2,1,0:T(2,128)(2,1)}, u32[]{:S(2)}, u32[]{:S(2)}) async-start(bf16[128,65,2,128]{3,2,1,0:T(2,128)(2,1)} %pack.1), calls=%async_computation | async-start | bytes 8519680 | tf_op jit(solution)/shard_map/all_to_all | solution.py:378
  26.6 0.0 copy-start.1
  26.6 0.0 copy-start.2
  26.7 0.0 copy-done
  26.8 1.0 fusion.16
  27.8 1.1 sine_convert_fusion
  29.0 1.0 fusion.15
  30.0 1.1 sine_convert_fusion.1
  31.2 0.1 pad_maximum_fusion.table_ref
  31.3 0.0 copy-done.1
  31.3 0.0 copy-done.2
  31.3 0.1 fusion.13
  31.4 93.6 %all-to-all-done = bf16[128,65,2,128]{3,2,1,0:T(2,128)(2,1)} async-done(((bf16[128,65,2,128]{3,2,1,0:T(2,128)(2,1)}), bf16[128,65,2,128]{3,2,1,0:T(2,128)(2,1)}, u32[]{:S(2)}, u32[]{:S(2)}) %all-to-all-start) | async-done | bytes 4259872 | tf_op jit(solution)/shard_map/all_to_all | solution.py:378
  125.0 17.0 %cells.1 = (bf16[32,2,128,128]{3,2,1,0:T(8,128)(2,1)}, f32[32,2,512]{2,1,0:T(2,128)S(1)}, f32[8,512]{1,0:T(8,128)S(1)}) custom-call(s32[1]{0:T(128)} %bitcast.at_ref, bf16[16640,128]{1,0:T(8,128)(2,1)} %bitcast.4.x_ref, f32[128,512]{1,0:T(8,128)S(1)} %get-tuple-element.52.valid_ref, bf16[2,512,512]{2,1,0:T(8,128)(2,1)S(1)} %pad_maximum_fusion.table_ref, ...), custom_call_target="tpu_custom_call" | custom-call | tf_op jit(solution)/shard_map/cells/pallas_call | solution.py:264
  142.0 0.4 collective-permute-start
  142.5 0.9 collective-permute-done
  143.4 11.4 %all_to_all.15 = f32[8,12,256]{2,1,0:T(8,128)S(1)} all-to-all(f32[8,12,256]{2,1,0:T(8,128)S(1)} %broadcast_in_dim.10), channel_id=1, replica_groups=mesh['slab'=2,'wide_0'=8,'wide_1'=8,'wide_2'=2] {'wide_1'}, dimensions={0} | all-to-all | bytes 196608 | tf_op jit(solution)/shard_map/all_to_all | solution.py:344
  154.8 27.4 %all_to_all.16 = f32[8,12,256]{2,1,0:T(8,128)S(1)} all-to-all(f32[8,12,256]{2,1,0:T(8,128)S(1)} %broadcast_in_dim.11), channel_id=1, replica_groups=mesh['slab'=2,'wide_0'=8,'wide_1'=8,'wide_2'=2] {'wide_0'}, dimensions={0} | all-to-all | bytes 196608 | tf_op jit(solution)/shard_map/all_to_all | solution.py:344
  182.4 3.5 %collective-permute-start.1 = (f32[2,3,256]{2,0,1:T(2,128)S(1)}, f32[2,3,256]{2,0,1:T(2,128)S(1)}, u32[]{:S(2)}, u32[]{:S(2)}) collective-permute-start(f32[2,3,256]{2,0,1:T(2,128)S(1)} %pad_maximum_fusion.1), channel_id=1, source_target_pairs={{0,1},{1,0},{2,3},{3,2},{4,5},{5,4},{6,7},{7,6},{8,9},{9,8},{10,11... | collective-permute-start | bytes 18440 | tf_op jit(solution)/shard_map/ppermute | solution.py:364
  185.9 0.8 collective-permute-done.1
  186.7 0.7 dynamic-slice_bitcast_fusion
  187.4 0.8 add_subtract_fusion
  (32 shorter events, 0.5 us)
Async XLA Ops:
  4.1 22.6 %copy-start = (s32[512,2]{0,1:T(2,128)S(1)}, s32[512,2]{0,1:T(2,128)}, u32[]{:S(2)}) copy-start(s32[512,2]{0,1:T(2,128)} %param.9) | copy-start | bytes 12292
  4.1 120.9 %all-to-all-start = ((bf16[128,65,2,128]{3,2,1,0:T(2,128)(2,1)}), bf16[128,65,2,128]{3,2,1,0:T(2,128)(2,1)}, u32[]{:S(2)}, u32[]{:S(2)}) async-start(bf16[128,65,2,128]{3,2,1,0:T(2,128)(2,1)} %pack.1), calls=%async_computation | async-start | bytes 8519680 | tf_op jit(solution)/shard_map/all_to_all | solution.py:378
  26.6 4.7 %copy-start.1 = (s32[128]{0:T(128)S(1)}, s32[128]{0:T(128)}, u32[]{:S(2)}) copy-start(s32[128]{0:T(128)} %param.8) | copy-start | bytes 1540
  26.6 4.7 %copy-start.2 = (s32[128]{0:T(128)S(1)}, s32[128]{0:T(128)}, u32[]{:S(2)}) copy-start(s32[128]{0:T(128)} %param.7) | copy-start | bytes 1540
  142.0 1.3 collective-permute-start
  182.4 4.4 %collective-permute-start.1 = (f32[2,3,256]{2,0,1:T(2,128)S(1)}, f32[2,3,256]{2,0,1:T(2,128)S(1)}, u32[]{:S(2)}, u32[]{:S(2)}) collective-permute-start(f32[2,3,256]{2,0,1:T(2,128)S(1)} %pad_maximum_fusion.1), channel_id=1, source_target_pairs={{0,1},{1,0},{2,3},{3,2},{4,5},{5,4},{6,7},{7,6},{8,9},{9,8},{10,11... | collective-permute-start | bytes 18440 | tf_op jit(solution)/shard_map/ppermute | solution.py:364

commit v3 on v2

--- a/solution.py
+++ b/solution.py
@@ -1,3 +1,4 @@
+import functools
 import math
 
 import jax
@@ -14,16 +15,17 @@
 LINE_CELLS = AZ // LOOK_AZ
 WIDE = ("wide_0", "wide_1", "wide_2")
 SLAB_WIDE = ("slab", "wide_0", "wide_1", "wide_2")
+SEND = ("wide_1", "wide_0", "wide_2")
 DAMPING = 1.0
 DATES_STEP = 32
 COLS_STEP = 8
 CELLS_STEP = 8
-ROT_ROWS = 32
 LANES = 128
 BLOCKS = AZ // LANES
 HALF = AZ // 2
+SCALE = 1.0 / AZ
 COL_ROWS = 2 * BLOCKS
-PACK_STEPS = 4
+SUBLANES = 8
 
 
 def bins_of(odd):
@@ -47,31 +49,30 @@
 
 
 def pack_kernel(samples_ref, offsets_ref, out_ref, buffer, own, extra_buffer, in_sem, out_sem):
-    devices, width = samples_ref.shape[:2]
-    share = devices // PACK_STEPS
-    rows = [pl.ds(i * share, share) for i in range(PACK_STEPS)]
+    major, minor, cores, width = samples_ref.shape[:4]
     ins = [
-        pltpu.make_async_copy(samples_ref.at[rows[i]], buffer.at[rows[i]], in_sem.at[i])
-        for i in range(PACK_STEPS)
+        pltpu.make_async_copy(samples_ref.at[:, i], buffer.at[i], in_sem.at[i])
+        for i in range(minor)
     ]
     outs = [
-        pltpu.make_async_copy(
-            buffer.at[rows[i]], out_ref.at[rows[i], pl.ds(0, width)], out_sem.at[i]
-        )
-        for i in range(PACK_STEPS)
+        pltpu.make_async_copy(buffer.at[i], out_ref.at[i, :, :, pl.ds(0, width)], out_sem.at[i])
+        for i in range(minor)
     ]
-    own_in = pltpu.make_async_copy(offsets_ref, own, in_sem.at[PACK_STEPS])
+    own_in = pltpu.make_async_copy(offsets_ref, own, in_sem.at[minor])
     own_in.start()
     for copy in ins:
         copy.start()
     own_in.wait()
-    sharing = devices * LANES // offsets_ref.shape[1]
-    for k in range(devices // sharing):
-        block = jnp.broadcast_to(own[:, k * LANES : (k + 1) * LANES], (2, LANES))
-        for i in range(sharing):
-            extra_buffer[k * sharing + i, 0] = block
+    here = offsets_ref.shape[1] // (major * minor * cores)
+    for x in range(major):
+        for y in range(minor):
+            for core in range(cores):
+                start = ((x * minor + y) * cores + core) * here // LANES * LANES
+                extra_buffer[y, x, core, 0] = jnp.broadcast_to(
+                    own[:, start : start + LANES], (2, LANES)
+                )
     extra = pltpu.make_async_copy(
-        extra_buffer, out_ref.at[:, pl.ds(width, 1)], out_sem.at[PACK_STEPS]
+        extra_buffer, out_ref.at[:, :, :, pl.ds(width, 1)], out_sem.at[minor]
     )
     extra.start()
     for copy_in, copy_out in zip(ins, outs):
@@ -83,18 +84,18 @@
 
 
 def packed(samples, offsets):
-    devices, width = samples.shape[:2]
+    major, minor, cores, width = samples.shape[:4]
     return pl.pallas_call(
         pack_kernel,
         in_specs=[pl.BlockSpec(memory_space=pl.ANY)] * 2,
         out_specs=pl.BlockSpec(memory_space=pl.ANY),
-        out_shape=jax.ShapeDtypeStruct((devices, width + 1, 2, LANES), samples.dtype),
+        out_shape=jax.ShapeDtypeStruct((minor, major, cores, width + 1, 2, LANES), samples.dtype),
         scratch_shapes=[
-            pltpu.VMEM(samples.shape, samples.dtype),
+            pltpu.VMEM((minor, major, cores, width, 2, LANES), samples.dtype),
             pltpu.VMEM(offsets.shape, offsets.dtype),
-            pltpu.VMEM((devices, 1, 2, LANES), samples.dtype),
-            pltpu.SemaphoreType.DMA((PACK_STEPS + 1,)),
-            pltpu.SemaphoreType.DMA((PACK_STEPS + 1,)),
+            pltpu.VMEM((minor, major, cores, 1, 2, LANES), samples.dtype),
+            pltpu.SemaphoreType.DMA((minor + 1,)),
+            pltpu.SemaphoreType.DMA((minor + 1,)),
         ],
         name="pack",
     )(samples, offsets)
@@ -113,8 +114,8 @@
 
 def turns(angle, lane):
     cos, sin = series(angle * jnp.where(lane == 0.0, HALF / 2.0, lane))
-    cos, sin = 1.0 - 2.0 * sin * sin, 2.0 * sin * cos
-    even_cos, even_sin = jnp.where(lane == 0.0, 1.0, cos), jnp.where(lane == 0.0, 0.0, sin)
+    cos, sin = SCALE - (2.0 * SCALE) * sin * sin, (2.0 * SCALE) * sin * cos
+    even_cos, even_sin = jnp.where(lane == 0.0, SCALE, cos), jnp.where(lane == 0.0, 0.0, sin)
     square = angle * angle
     one_cos, one_sin = 1.0 - square * (0.5 - square * (1.0 / 24)), angle - angle * square * (1.0 / 6)
     odd_cos = even_cos * one_cos - even_sin * one_sin
@@ -123,7 +124,7 @@
 
 
 def cells_kernel(
-    at_ref, x_ref, valid_ref, table_ref, second_ref, first_ref, coh_ref, ifg_ref, sums_ref,
+    major, cores, at_ref, x_ref, valid_ref, table_ref, second_ref, first_ref, coh_ref, ifg_ref, sums_ref,
     wide_ref, spec_ref, angle_ref, turned_ref, pix_ref, gamma_ref, int_ref,
 ):
     step = pl.program_id(0)
@@ -136,14 +137,27 @@
     def _forward():
         wide_ref[...] = x_ref[...].astype(jnp.float32)
         valid = valid_ref[...]
-        shifts = wide_ref[pl.ds(LOOK_RG * COL_ROWS, DATES_STEP, stride=stride), :]
+
+        def rows_of(offset):
+            return jnp.concatenate(
+                [
+                    wide_ref[
+                        pl.ds((y * major * cores + core) * stride + offset, major, stride=cores * stride), :
+                    ]
+                    for y in range(DATES_STEP // (major * cores))
+                    for core in range(cores)
+                ],
+                0,
+            )
+
+        shifts = rows_of(LOOK_RG * COL_ROWS)
         shifts = pltpu.roll(shifts, at_ref[0], 1)
         for c in range(LOOK_RG):
             sums, differences = [], []
             for part in range(2):
                 for block in range(BLOCKS // 2):
                     low, high = (
-                        wide_ref[pl.ds(c * COL_ROWS + 2 * b + part, DATES_STEP, stride=stride), :]
+                        rows_of(c * COL_ROWS + 2 * b + part)
                         * valid[:, b * LANES : (b + 1) * LANES]
                         for b in (block, block + BLOCKS // 2)
                     )
@@ -160,39 +174,46 @@
                 spec_ref[:, at], table_ref[odd], preferred_element_type=jnp.float32
             ).astype(jnp.bfloat16)
         lane = lax.broadcasted_iota(jnp.int32, (1, LANES), 1).astype(jnp.float32)
-        groups = DATES_STEP // ROT_ROWS
-
-        def turn(i, _):
-            rows = pl.ds(pl.multiple_of(i * ROT_ROWS, ROT_ROWS), ROT_ROWS)
-            column, group = i // groups, i % groups
-            target = pl.ds(
-                pl.multiple_of(column * dates + step * DATES_STEP + group * ROT_ROWS, ROT_ROWS),
-                ROT_ROWS,
-            )
+
+        def turn(column, _):
+            rows = pl.ds(pl.multiple_of(column * DATES_STEP, DATES_STEP), DATES_STEP)
+            first_row = column * dates + step * (DATES_STEP // major)
             for block, (cos, sin) in enumerate(turns(angle_ref[rows, :], lane)):
                 start = (block // 2) * AZ + (block % 2) * LANES
                 at, at_imag = slice(start, start + LANES), slice(start + HALF, start + HALF + LANES)
                 real = spec_ref[rows, at].astype(jnp.float32)
                 imag = spec_ref[rows, at_imag].astype(jnp.float32)
-                turned_ref[target, at] = (real * cos - imag * sin).astype(jnp.bfloat16)
-                turned_ref[target, at_imag] = (real * sin + imag * cos).astype(jnp.bfloat16)
+                turned_real, turned_imag = real * cos - imag * sin, real * sin + imag * cos
+                for k in range(DATES_STEP // major):
+                    for first_lane, turned in ((start, turned_real), (start + HALF, turned_imag)):
+                        row = first_lane // LANES * (LOOK_RG * dates) + first_row + k
+                        turned_ref[pl.ds(row, major, stride=dates // major), :] = turned[
+                            k * major : (k + 1) * major
+                        ]
             return _
 
-        lax.fori_loop(0, LOOK_RG * groups, turn, None)
+        lax.fori_loop(0, LOOK_RG, turn, None)
 
     @pl.when((step >= date_steps) & (step < date_steps + range_steps))
     def _inverse():
         first_column = (step - date_steps) * COLS_STEP
-        rows = pl.ds(pl.multiple_of(first_column * dates, COLS_STEP * dates), COLS_STEP * dates)
+
+        def turned_rows(block):
+            start = block * (LOOK_RG * dates) + first_column * dates
+            rows = pl.ds(pl.multiple_of(start, COLS_STEP * dates), COLS_STEP * dates)
+            return turned_ref[rows, :].astype(jnp.bfloat16)
+
         even, odd = (
             lax.dot_general(
-                table_ref[k], turned_ref[rows, k * AZ : (k + 1) * AZ], (((1,), (1,)), ((), ())),
+                table_ref[k],
+                jnp.concatenate([turned_rows(k * BLOCKS + b) for b in range(BLOCKS)], 1),
+                (((1,), (1,)), ((), ())),
                 preferred_element_type=jnp.float32,
             )
             for k in range(2)
         )
         for half, restored in enumerate((even + odd, even - odd)):
-            restored = (restored * (1.0 / AZ)).astype(jnp.bfloat16)
+            restored = restored.astype(jnp.bfloat16)
             cells = slice(half * LINE_CELLS // 2, (half + 1) * LINE_CELLS // 2)
             for c in range(COLS_STEP):
                 pix_ref[:, cells, first_column + c] = restored[
@@ -222,8 +243,7 @@
                 high = gamma.astype(jnp.bfloat16)
                 coh_ref[k, part] = high
                 rows = slice((2 * k + part) * dates, (2 * k + part + 1) * dates)
-                gamma_ref[rows, :dates] = high
-                gamma_ref[rows, dates:] = (gamma - high.astype(jnp.float32)).astype(jnp.bfloat16)
+                gamma_ref[rows, :] = high
         picked = jnp.dot(gamma_ref[...], second_ref[...], preferred_element_type=jnp.float32)
         first = first_ref[...]
         for k in range(CELLS_STEP):
@@ -250,7 +270,7 @@
         sums_ref[len(terms) :, :] = jnp.zeros_like(sums_ref[len(terms) :, :])
 
 
-def cells_call(at, x, valid, table, second, first):
+def cells_call(major, cores, at, x, valid, table, second, first):
     dates, pairs = first.shape
     date_steps = dates // DATES_STEP
     before = date_steps + LOOK_RG // COLS_STEP
@@ -262,7 +282,7 @@
         return pl.BlockSpec(shape, lambda s: (0,) * len(shape))
 
     return pl.pallas_call(
-        cells_kernel,
+        functools.partial(cells_kernel, major, cores),
         grid=(steps,),
         in_specs=[
             pl.BlockSpec(memory_space=pltpu.SMEM),
@@ -288,9 +308,9 @@
             pltpu.VMEM((DATES_STEP * stride, LANES), jnp.float32),
             pltpu.VMEM((LOOK_RG * DATES_STEP, 2 * AZ), jnp.bfloat16),
             pltpu.VMEM((LOOK_RG * DATES_STEP, LANES), jnp.float32),
-            pltpu.VMEM((LOOK_RG * dates, 2 * AZ), jnp.bfloat16),
+            pltpu.VMEM((2 * BLOCKS * LOOK_RG * dates, LANES), jnp.float32),
             pltpu.VMEM((2, LINE_CELLS, LOOK_RG, LOOK_AZ, dates), jnp.bfloat16),
-            pltpu.VMEM((2 * CELLS_STEP * dates, 2 * dates), jnp.bfloat16),
+            pltpu.VMEM((2 * CELLS_STEP * dates, dates), jnp.bfloat16),
             pltpu.VMEM((LINE_CELLS, 2, pairs), jnp.float32),
         ],
         compiler_params=pltpu.CompilerParams(
@@ -374,16 +394,18 @@
     here = columns // devices
     dates = devices * slc.shape[0]
     at = (LANES - here * (position % (LANES // here))) % LANES
-    sent = packed(line_blocks(slc.reshape(devices, here, 2, AZ)), offsets)
-    received = lax.all_to_all(sent, WIDE, 0, 0, tiled=True)
+    major, minor, cores = (lax.axis_size(axis) for axis in WIDE)
+    samples = line_blocks(slc.reshape(devices, here, 2, AZ))
+    sent = packed(samples.reshape(major, minor, cores, *samples.shape[1:]), offsets)
+    received = lax.all_to_all(sent.reshape(devices, *sent.shape[3:]), SEND, 0, 0, tiled=True)
     lines = jnp.arange(AZ, dtype=jnp.int32)[None, :]
     valid = ((lines >= row_start[:, None]) & (lines < row_stop[:, None])).astype(jnp.float32)
+    valid = valid.reshape(major, minor, cores, AZ).transpose(1, 2, 0, 3).reshape(dates, AZ)
     date = jnp.arange(dates, dtype=jnp.int32)[:, None]
     first = (date == pairs[:, 0][None, :]).astype(jnp.float32)
     second = (date == pairs[:, 1][None, :]).astype(jnp.bfloat16)
-    second = jnp.concatenate([second, second], 0)
     coherence, ifg, sums = cells_call(
-        at.reshape(1), received.reshape(-1, LANES), valid, spectral_tables(), second, first
+        major, cores, at.reshape(1), received.reshape(-1, LANES), valid, spectral_tables(), second, first
     )
 
     range_cells = columns // LOOK_RG

time: 189 us -> 186 us (0.984)
  blocking collectives: 38.7 us -> 34.5 us
  waiting for transfers between devices: 95.3 us -> 92.6 us
    all_to_all x2, blocking collectives: 38.7 us -> 34.5 us  [summed_over(): return jnp.sum(lax.all_to_all(copies, axis, 0, 0, tiled=True), 0)]
    all_to_all x1, waiting for transfers between devices: 93.6 us -> 91 us  [local(): lax.all_to_all(sent.reshape(devices, *sent.shape[3:]), SEND, 0, 0, tiled=...]
  transfers between devices with their start and end apart: 3 -> 3, of which waited for: 3 -> 3; matrix products, arithmetic and copies ran while one was open for 2% -> 3% of each run, Pallas kernels for 0% -> 0%
where the time goes in v3:
time: 186 us; the launch traced here: 184 us
  waiting for transfers between devices  92.6 us (50%)
  blocking collectives  34.5 us (19%)
  starting transfers between devices  27.5 us (15%)
  Pallas kernels  20.9 us (11%)
  other arithmetic  5.53 us (3%)
    all_to_all x1, waiting for transfers between devices, local(): lax.all_to_all(sent.reshape(devices, *sent.shape[3:]), SEND, 0, 0, tiled=...  91 us
    all_to_all x2, blocking collectives, summed_over(): return jnp.sum(lax.all_to_all(copies, axis, 0, 0, tiled=True), 0)  34.5 us
    all_to_all x1, starting transfers between devices, local(): lax.all_to_all(sent.reshape(devices, *sent.shape[3:]), SEND, 0, 0, tiled=...  22.5 us
    pallas_call x1, Pallas kernels, cells_call(): pl.pallas_call(functools.partial(cells_kernel, major, cores), grid=(steps...  17.2 us
    pallas_call x1, Pallas kernels, packed(): pl.pallas_call(pack_kernel, in_specs=[pl.BlockSpec(memory_space=pl.ANY)]...  3.76 us
  transfers between devices with their start and end apart: 3, of which 3 were waited for; matrix products, arithmetic and copies ran while one was open for 3% of the time, Pallas kernels for 0%

profile of v3, /device:TPU:641, one launch (start us, length us, event | category | flops | bytes accessed | tf_op | source)
XLA Modules:
  0.0 183.5 jit_solution(14240049778453186032)
XLA Ops:
  0.6 3.8 %pack.1 = bf16[8,8,2,65,2,128]{5,4,3,2,1,0:T(2,128)(2,1)} custom-call(bf16[8,8,2,64,2,128]{5,4,3,2,1,0:T(2,128)(2,1)} %bitcast.60, bf16[1,2048]{1,0:T(2,128)(2,1)} %offsets_ref.1), custom_call_target="tpu_custom_call" | custom-call | tf_op jit(solution)/shard_map/pack/pallas_call | solution.py:88
  4.4 0.0 copy-start.1
  4.4 0.0 copy-start.2
  4.4 22.5 %all-to-all-start = ((bf16[128,65,2,128]{3,2,1,0:T(2,128)(2,1)}), bf16[128,65,2,128]{3,2,1,0:T(2,128)(2,1)}, u32[]{:S(2)}, u32[]{:S(2)}) async-start(bf16[128,65,2,128]{3,2,1,0:T(2,128)(2,1)} %bitcast.59), calls=%async_computation | async-start | bytes 8519680 | tf_op jit(solution)/shard_map/all_to_all | solution.py:400
  26.9 0.0 copy-start
  27.0 0.0 copy-done.1
  27.0 0.1 lt.45
  27.1 0.1 copy.19
  27.2 0.1 lt.47
  27.3 0.0 copy-done.2
  27.3 0.1 ge.25
  27.5 0.1 copy.18
  27.6 0.1 ge.27
  27.8 1.0 fusion.17
  28.8 1.1 sine_convert_fusion
  30.0 1.0 fusion.16
  31.0 1.1 sine_convert_fusion.1
  32.1 0.1 pad_maximum_fusion.table_ref
  32.2 0.0 copy-done
  32.3 0.1 fusion.13
  32.4 91.0 %all-to-all-done = bf16[128,65,2,128]{3,2,1,0:T(2,128)(2,1)} async-done(((bf16[128,65,2,128]{3,2,1,0:T(2,128)(2,1)}), bf16[128,65,2,128]{3,2,1,0:T(2,128)(2,1)}, u32[]{:S(2)}, u32[]{:S(2)}) %all-to-all-start) | async-done | bytes 4259872 | tf_op jit(solution)/shard_map/all_to_all | solution.py:400
  123.4 17.2 %cells.1 = (bf16[32,2,128,128]{3,2,1,0:T(8,128)(2,1)}, f32[32,2,512]{2,1,0:T(2,128)S(1)}, f32[8,512]{1,0:T(8,128)S(1)}) custom-call(s32[1]{0:T(128)} %bitcast.at_ref, bf16[16640,128]{1,0:T(8,128)(2,1)} %bitcast.5.x_ref, f32[128,512]{1,0:T(8,128)S(1)} %get-tuple-element.52.valid_ref, bf16[2,512,512]{2,1,0:T(8,128)(2,1)S(1)} %pad_maximum_fusion.table_ref, ...), custom_call_target="tpu_custom_call" | custom-call | tf_op jit(solution)/shard_map/cells/pallas_call | solution.py:284
  140.6 1.5 collective-permute-start
  142.2 0.8 collective-permute-done
  143.0 11.5 %all_to_all.15 = f32[8,12,256]{2,1,0:T(8,128)S(1)} all-to-all(f32[8,12,256]{2,1,0:T(8,128)S(1)} %broadcast_in_dim.10), channel_id=1, replica_groups=mesh['slab'=2,'wide_0'=8,'wide_1'=8,'wide_2'=2] {'wide_1'}, dimensions={0} | all-to-all | bytes 196608 | tf_op jit(solution)/shard_map/all_to_all | solution.py:364
  154.6 22.9 %all_to_all.16 = f32[8,12,256]{2,1,0:T(8,128)S(1)} all-to-all(f32[8,12,256]{2,1,0:T(8,128)S(1)} %broadcast_in_dim.11), channel_id=1, replica_groups=mesh['slab'=2,'wide_0'=8,'wide_1'=8,'wide_2'=2] {'wide_0'}, dimensions={0} | all-to-all | bytes 196608 | tf_op jit(solution)/shard_map/all_to_all | solution.py:364
  177.7 3.5 %collective-permute-start.1 = (f32[2,3,256]{2,0,1:T(2,128)S(1)}, f32[2,3,256]{2,0,1:T(2,128)S(1)}, u32[]{:S(2)}, u32[]{:S(2)}) collective-permute-start(f32[2,3,256]{2,0,1:T(2,128)S(1)} %pad_maximum_fusion.1), channel_id=1, source_target_pairs={{0,1},{1,0},{2,3},{3,2},{4,5},{5,4},{6,7},{7,6},{8,9},{9,8},{10,11... | collective-permute-start | bytes 18440 | tf_op jit(solution)/shard_map/ppermute | solution.py:384
  181.2 0.8 collective-permute-done.1
  182.1 0.7 dynamic-slice_bitcast_fusion
  182.7 0.8 add_subtract_fusion
  (31 shorter events, 0.4 us)
Async XLA Ops:
  4.4 22.6 %copy-start.1 = (s32[128]{0:T(128)S(1)}, s32[128]{0:T(128)}, u32[]{:S(2)}) copy-start(s32[128]{0:T(128)} %param.8) | copy-start | bytes 1540
  4.4 22.9 %copy-start.2 = (s32[128]{0:T(128)S(1)}, s32[128]{0:T(128)}, u32[]{:S(2)}) copy-start(s32[128]{0:T(128)} %param.7) | copy-start | bytes 1540
  4.4 118.9 %all-to-all-start = ((bf16[128,65,2,128]{3,2,1,0:T(2,128)(2,1)}), bf16[128,65,2,128]{3,2,1,0:T(2,128)(2,1)}, u32[]{:S(2)}, u32[]{:S(2)}) async-start(bf16[128,65,2,128]{3,2,1,0:T(2,128)(2,1)} %bitcast.59), calls=%async_computation | async-start | bytes 8519680 | tf_op jit(solution)/shard_map/all_to_all | solution.py:400
  26.9 5.3 %copy-start = (s32[512,2]{0,1:T(2,128)S(1)}, s32[512,2]{0,1:T(2,128)}, u32[]{:S(2)}) copy-start(s32[512,2]{0,1:T(2,128)} %param.9) | copy-start | bytes 12292
  140.6 2.4 %collective-permute-start = (f32[8,256]{1,0:T(8,128)S(1)}, f32[8,256]{1,0:T(8,128)S(1)}, u32[]{:S(2)}, u32[]{:S(2)}) collective-permute-start(f32[8,256]{1,0:T(8,128)S(1)} %get-tuple-element.18), channel_id=1, source_target_pairs={{0,1},{1,0},{2,3},{3,2},{4,5},{5,4},{6,7},{7,6},{8,9},{9,8},{10,11... | collective-permute-start | bytes 24584 | tf_op jit(solution)/shard_map/ppermute | solution.py:379
  177.7 4.4 %collective-permute-start.1 = (f32[2,3,256]{2,0,1:T(2,128)S(1)}, f32[2,3,256]{2,0,1:T(2,128)S(1)}, u32[]{:S(2)}, u32[]{:S(2)}) collective-permute-start(f32[2,3,256]{2,0,1:T(2,128)S(1)} %pad_maximum_fusion.1), channel_id=1, source_target_pairs={{0,1},{1,0},{2,3},{3,2},{4,5},{5,4},{6,7},{7,6},{8,9},{9,8},{10,11... | collective-permute-start | bytes 18440 | tf_op jit(solution)/shard_map/ppermute | solution.py:384
